TPU v7x, 128 devices: a whole 4x4x4 slice. The times are simulated.
128 devices in a mesh: gx: 4 (over x), gz: 4 (over y_lo, core), ta: 8 (over z, y_hi).
Axes of the slice: x: 4, y: 4 (y_hi: 2, y_lo: 2; y = y_hi * 2 + y_lo), z: 4, core: 2. Of those that a mesh axis runs over, the one named last changes fastest.
Arguments:
- propagator: float32 [2, 12, 12, 1048576], P(None, None, None, ('gx', 'gz', 'ta')), may hold values from -6 to 6
- momenta: int32 [512, 4], P(('gx', 'gz', 'ta')), may hold values from -16 to 15
- gamma_index: int32 [16], replicated, may hold values from 0 to 15, each once
Outputs:
- vertices: float32 [512, 16, 2, 12, 12], P(('gx', 'gz', 'ta'))
Inputs may be any that keep to these rules, and one draw needn't show every extreme that they name: `momenta`: A momentum component enters only modulo the lattice length along its direction. `gamma_index`: every mask of 0 to 15 appears once.
All inputs are finite; a program needn't handle non-finite values.
Results may differ from a plain program's by a relative error of at most 0.0001.
Values sent between devices are 32-bit elements; how exact they have to be, the bound alone decides.
A program may use at most 128 MiB of HBM per device.

v0:
```python
import math

import jax
import jax.numpy as jnp
import numpy as np
from jax import lax
from jax.sharding import PartitionSpec as P

LX = 32
LY = 32
LZ = 32
LT = 32


def in_blocks(array, dim, devices):
    before, after = (array.shape[:dim], array.shape[dim + 1 :])
    return jnp.moveaxis(array.reshape(*before, devices, -1, *after), dim, 0)


def summed_on_arrival(array, axis, dim):
    devices = lax.axis_size(axis)
    blocks = lax.all_to_all(in_blocks(array, dim, devices), axis, 0, 0, tiled=True)
    return jnp.sum(blocks, axis=0)


def clifford_table():
    zeros = np.zeros((4, 4))
    first = (zeros, np.array([[0, 0, 0, 1], [0, 0, 1, 0], [0, -1, 0, 0], [-1, 0, 0, 0]]))
    second = (np.array([[0, 0, 0, -1], [0, 0, 1, 0], [0, 1, 0, 0], [-1, 0, 0, 0]]), zeros)
    third = (zeros, np.array([[0, 0, 1, 0], [0, 0, 0, -1], [-1, 0, 0, 0], [0, 1, 0, 0]]))
    fourth = (np.array([[0, 0, 1, 0], [0, 0, 0, 1], [1, 0, 0, 0], [0, 1, 0, 0]]), zeros)
    basis = [first, second, third, fourth]
    tables_re = []
    tables_im = []
    for mask in range(16):
        matrix_re = np.identity(4)
        matrix_im = np.zeros((4, 4))
        for bit in range(4):
            if mask >> bit & 1:
                basis_re, basis_im = basis[bit]
                new_re = matrix_re @ basis_re - matrix_im @ basis_im
                new_im = matrix_re @ basis_im + matrix_im @ basis_re
                matrix_re, matrix_im = (new_re, new_im)
        tables_re.append(matrix_re)
        tables_im.append(matrix_im)
    return (np.stack(tables_re), np.stack(tables_im))


def select_gammas(gamma_index):
    table_re, table_im = clifford_table()
    onehot = (gamma_index[:, None] == jnp.arange(16, dtype=jnp.int32)[None, :]).astype(jnp.float32)
    high = lax.Precision.HIGHEST
    chosen_re = jnp.einsum(
        "gk,kst->gst", onehot, jnp.asarray(table_re, jnp.float32), precision=high
    )
    chosen_im = jnp.einsum(
        "gk,kst->gst", onehot, jnp.asarray(table_im, jnp.float32), precision=high
    )
    return (chosen_re, chosen_im)


def vertices_of(spec_re, spec_im, gamma_re, gamma_im):
    high = lax.Precision.HIGHEST
    count = spec_re.shape[0]
    split_re = spec_re.reshape(count, 4, 3, 12)
    split_im = spec_im.reshape(count, 4, 3, 12)
    turned_re = (
        jnp.einsum("gst,mtcb->mgscb", gamma_re, split_re, precision=high)
        - jnp.einsum("gst,mtcb->mgscb", gamma_im, split_im, precision=high)
    ).reshape(count, 16, 12, 12)
    turned_im = (
        jnp.einsum("gst,mtcb->mgscb", gamma_re, split_im, precision=high)
        + jnp.einsum("gst,mtcb->mgscb", gamma_im, split_re, precision=high)
    ).reshape(count, 16, 12, 12)
    result_re = jnp.einsum("mka,mgkb->mgab", spec_re, turned_re, precision=high) + jnp.einsum(
        "mka,mgkb->mgab", spec_im, turned_im, precision=high
    )
    result_im = jnp.einsum("mka,mgkb->mgab", spec_re, turned_im, precision=high) - jnp.einsum(
        "mka,mgkb->mgab", spec_im, turned_re, precision=high
    )
    return jnp.stack([result_re, result_im], axis=2)


def site_coordinates(local_sites):
    block_x = LX // lax.axis_size("gx")
    block_z = LZ // lax.axis_size("gz")
    block_t = LT // lax.axis_size("ta")
    linear = jnp.arange(local_sites, dtype=jnp.int32)
    coord_t = linear % block_t + lax.axis_index("ta") * block_t
    coord_z = linear // block_t % block_z + lax.axis_index("gz") * block_z
    coord_y = linear // (block_t * block_z) % LY
    coord_x = linear // (block_t * block_z * LY) + lax.axis_index("gx") * block_x
    return jnp.stack([coord_x, coord_y, coord_z, coord_t])


def make_term(momentum_rows, coords, plain_re, diff_part, summed_part):
    lengths = (LX, LY, LZ, LT)
    common = lengths[0]
    for length in lengths[1:]:
        common = common * length // math.gcd(common, length)
    high = lax.Precision.HIGHEST

    def single_block(waves):
        phase_index = jnp.zeros((waves.shape[0], coords.shape[1]), jnp.int32)
        for direction in range(4):
            reduced = waves[:, direction] % lengths[direction] * (common // lengths[direction])
            phase_index = phase_index + reduced[:, None] * coords[direction][None, :]
        phase_index = phase_index % common
        angle = phase_index.astype(jnp.float32) * (2.0 * math.pi / float(common))
        cosine = jnp.cos(angle)
        sine = jnp.sin(angle)
        first = jnp.einsum("ms,cs->mc", cosine - sine, plain_re, precision=high)
        second = jnp.einsum("ms,cs->mc", cosine, diff_part, precision=high)
        third = jnp.einsum("ms,cs->mc", -sine, summed_part, precision=high)
        return jnp.concatenate([first - third, first + second], axis=1)

    def term(start, count):
        width = math.gcd(count, 512)
        picked = momentum_rows
        picked = picked.reshape(count // width, width, 4)
        return lax.map(single_block, picked).reshape(count, 288)

    return term


def body(propagator, momenta, gamma_index):
    local_sites = propagator.shape[3]
    mine = momenta.shape[0]
    coords = site_coordinates(local_sites)
    plain_re = propagator[0].reshape(144, local_sites)
    plain_im = propagator[1].reshape(144, local_sites)
    diff_part = plain_im - plain_re
    summed_part = plain_re + plain_im
    gathered = lax.all_gather(momenta, ("gx", "gz", "ta"), axis=0, tiled=True)
    spatial = lax.axis_size("gx") * lax.axis_size("gz")
    ordered = gathered.reshape(spatial, lax.axis_size("ta"), mine, 4)
    ordered = jnp.transpose(ordered, (1, 0, 2, 3)).reshape(-1, 4)
    term = make_term(ordered, coords, plain_re, diff_part, summed_part)
    partial_value = summed_on_arrival(
        term(jnp.int32(0), spatial * mine * lax.axis_size("ta")), "ta", 0
    )
    spectrum = summed_on_arrival(partial_value, ("gx", "gz"), 0)
    spectrum = spectrum * (1.0 / math.sqrt(float(LX * LY * LZ * LT)))
    spectrum = spectrum.reshape(mine, 2, 12, 12)
    gamma_re, gamma_im = select_gammas(gamma_index)
    return vertices_of(spectrum[:, 0], spectrum[:, 1], gamma_re, gamma_im)


def solution(mesh):
    placed = (P(None, None, None, ("gx", "gz", "ta")), P(("gx", "gz", "ta"), None), P())
    return jax.shard_map(
        body,
        mesh=mesh,
        in_specs=placed,
        out_specs=P(("gx", "gz", "ta"), None, None, None, None),
        check_vma=False,
    )
```

profile of v0, /device:TPU:1, one launch (start us, length us, event | category | flops | bytes accessed | tf_op | source)
XLA Modules:
  0.0 679.2 jit_solution(13706072542922024557)
XLA Ops:
  0.0 32.7 %slice_reduce_fusion = (f32[12,12,8192]{2,1,0:T(8,128)}, f32[12,12,8192]{2,1,0:T(8,128)}) fusion(f32[2,12,12,8192]{3,0,2,1:T(2,128)} %param.5), kind=kLoop, calls=%fused_computation.15 | loop fusion | bytes 18874368 | tf_op jit(solution)/shard_map/slice | solution.py:131
  32.7 6.0 reshape_squeeze.12
  38.7 6.0 reshape_squeeze.13
  44.7 6.9 %fusion.108 = f32[144,8192]{1,0:T(8,128)} fusion(f32[144,8192]{1,0:T(8,128)} %reshape_squeeze.13, f32[144,8192]{1,0:T(8,128)} %reshape_squeeze.12), kind=kLoop, calls=%fused_computation.13.clone.clone.clone.2 | loop fusion | flops 1179648 | bytes 14155776 | tf_op jit(solution)/shard_map/while/body/eval_jaxpr/ms,cs->mc/dot_general | solution.py:113
  51.6 1.2 copy-done
  52.8 3.0 fusion.110
  55.8 310.6 %all-gather = s32[128,4,4]{2,1,0:T(4,128)S(1)} all-gather(s32[1,4,4]{2,1,0:T(4,128)S(1)} %bitcast.115), channel_id=1, replica_groups=mesh['gx'=4,'gz'=4,'ta'=8] {'gx','gz','ta'}, dimensions={0}, use_global_device_ids=true | all-gather | bytes 8256 | tf_op jit(solution)/shard_map/all_gather | solution.py:134
  366.4 1.0 copy.58
  367.7 72.3 %fusion.106 = f32[512,8192]{1,0:T(8,128)} fusion(s32[8192]{0:T(1024)S(1)} %get-tuple-element.46, s32[512]{0:T(512)S(1)} %bitcast.106, s32[8192]{0:T(1024)S(1)} %get-tuple-element.45, s32[512]{0:T(512)S(1)} %bitcast.109, s32[8192]{0:T(1024)S(1)} %get-tuple-element.42, s32[512]{0:T(512)S(1)} %bitcast.112, s32[8192]{0:T(1024)S(1)} %get-tuple-element.44, ...), kind=kLoop, calls=%fused_computation.9.clone.1 | loop fusion | flops 88080384 | bytes 16916480 | tf_op jit(solution)/shard_map/while/body/eval_jaxpr/ms,cs->mc/dot_general | solution.py:112
  440.0 20.4 %fusion.5 = f32[512,144]{0,1:T(8,128)S(1)} fusion(f32[144,8192]{1,0:T(8,128)S(1)} %bitcast.86, f32[512,8192]{1,0:T(8,128)} %fusion.106), kind=kOutput, calls=%fused_computation.8 | convolution fusion | flops 7247757312 | bytes 21790720 | tf_op jit(solution)/shard_map/while/body/eval_jaxpr/ms,cs->mc/dot_general | solution.py:112
  460.5 80.0 %fusion.20 = f32[512,144]{0,1:T(8,128)S(1)} fusion(f32[512,144]{0,1:T(8,128)S(1)} %fusion.5, s32[8192]{0:T(1024)S(1)} %get-tuple-element.46, s32[512]{0:T(512)S(1)} %bitcast.107, s32[8192]{0:T(1024)S(1)} %get-tuple-element.45, s32[512]{0:T(512)S(1)} %bitcast.110, s32[8192]{0:T(1024)S(1)} %get-tuple-element.42, s32[512]{0:T(512)S(1)} %bitcast.113, ...), kind=kOutput, calls=%fused_computation.25 | convolution fusion | flops 7331717120 | bytes 5447680 | tf_op jit(solution)/shard_map/while/body/eval_jaxpr/ms,cs->mc/dot_general | solution.py:113
  540.6 94.9 %fusion.25 = f32[512,144]{0,1:T(8,128)S(1)} fusion(f32[512,144]{0,1:T(8,128)S(1)} %fusion.5, s32[8192]{0:T(1024)S(1)} %get-tuple-element.46, s32[512]{0:T(512)S(1)} %bitcast.108, s32[8192]{0:T(1024)S(1)} %get-tuple-element.45, s32[512]{0:T(512)S(1)} %bitcast.111, s32[8192]{0:T(1024)S(1)} %get-tuple-element.42, s32[512]{0:T(512)S(1)} %bitcast.114, ...), kind=kOutput, calls=%fused_computation.26 | convolution fusion | flops 7335911424 | bytes 5447680 | tf_op jit(solution)/shard_map/while/body/eval_jaxpr/ms,cs->mc/dot_general | solution.py:114
  635.5 1.2 copy.59
  636.7 3.5 all-to-all-start
  640.2 0.2 fusion.61
  640.4 10.2 %all-to-all-done = f32[8,64,288]{2,1,0:T(8,128)S(1)} async-done(((f32[8,64,288]{2,1,0:T(8,128)}), f32[8,64,288]{2,1,0:T(8,128)S(1)}, u32[]{:S(2)}, u32[]{:S(2)}) %all-to-all-start) | async-done | bytes 589856 | tf_op jit(solution)/shard_map/all_to_all | solution.py:22
  650.6 0.7 reshape.89
  651.3 14.7 %all-to-all-start.1 = ((f32[16,4,288]{2,1,0:T(4,128)}), f32[16,4,288]{2,1,0:T(4,128)S(1)}, u32[]{:S(2)}, u32[]{:S(2)}) async-start(f32[16,4,288]{2,1,0:T(4,128)} %reshape.89), calls=%async_computation.1 | async-start | bytes 196608 | tf_op jit(solution)/shard_map/all_to_all | solution.py:22
  666.2 5.8 all-to-all-done.1
  672.2 0.6 fusion.54
  672.7 0.6 fusion.58
  673.3 0.6 fusion.18
  673.9 0.2 copy.71
  674.1 0.4 copy.72
  674.4 0.5 fusion.46
  674.9 0.6 fusion.19
  675.5 0.2 copy.67
  675.7 0.4 copy.68
  676.0 0.5 fusion.48
  676.5 0.5 fusion.16
  677.0 0.5 fusion.17
  677.5 1.5 copy.75
  (43 shorter events, 0.8 us)
Async XLA Ops:
  38.7 12.9 %slice-start = ((s8[4718592]{0:T(1024)(128)(4,1)}), s8[524288]{0:T(1024)(128)(4,1)S(1)}, s32[]{:S(2)}) async-start(s8[4718592]{0:T(1024)(128)(4,1)} %bitcast.83), calls=%async_computation.2 | async-start | bytes 1048576
  44.7 6.9 %slice-start.1 = ((s8[4718592]{0:T(1024)(128)(4,1)}), s8[4194304]{0:T(1024)(128)(4,1)S(1)}, s32[]{:S(2)}) async-start(s8[4718592]{0:T(1024)(128)(4,1)} %bitcast.83), calls=%async_computation.3 | async-start | bytes 8388608
  44.7 8.1 %copy-start = (f32[144,8192]{1,0:T(8,128)S(1)}, f32[144,8192]{1,0:T(8,128)}, u32[]{:S(2)}) copy-start(f32[144,8192]{1,0:T(8,128)} %reshape_squeeze.13) | copy-start | bytes 14155780
  44.7 11.1 %copy-start.1 = (s32[4,4]{1,0:T(4,128)S(1)}, s32[4,4]{1,0:T(4,128)}, u32[]{:S(2)}) copy-start(s32[4,4]{1,0:T(4,128)} %param.6) | copy-start | bytes 196
  52.8 387.2 %slice-start.2 = ((s8[4718592]{0:T(1024)(128)(4,1)}), s8[524288]{0:T(1024)(128)(4,1)S(1)}, s32[]{:S(2)}) async-start(s8[4718592]{0:T(1024)(128)(4,1)} %bitcast.85), calls=%async_computation.4 | async-start | bytes 1048576
  367.7 72.3 %slice-start.3 = ((s8[4718592]{0:T(1024)(128)(4,1)}), s8[4194304]{0:T(1024)(128)(4,1)S(1)}, s32[]{:S(2)}) async-start(s8[4718592]{0:T(1024)(128)(4,1)} %bitcast.85), calls=%async_computation.5 | async-start | bytes 8388608
  367.7 92.8 %slice-start.6 = ((s8[4718592]{0:T(1024)(128)(4,1)}), s8[4194304]{0:T(1024)(128)(4,1)S(1)}, s32[]{:S(2)}) async-start(s8[4718592]{0:T(1024)(128)(4,1)} %bitcast.89), calls=%async_computation.8 | async-start | bytes 8388608
  440.0 20.5 %slice-start.7 = ((s8[4718592]{0:T(1024)(128)(4,1)}), s8[524288]{0:T(1024)(128)(4,1)S(1)}, s32[]{:S(2)}) async-start(s8[4718592]{0:T(1024)(128)(4,1)} %bitcast.89), calls=%async_computation.9 | async-start | bytes 1048576
  440.0 100.5 %slice-start.4 = ((s8[4718592]{0:T(1024)(128)(4,1)}), s8[524288]{0:T(1024)(128)(4,1)S(1)}, s32[]{:S(2)}) async-start(s8[4718592]{0:T(1024)(128)(4,1)} %bitcast.87), calls=%async_computation.6 | async-start | bytes 1048576
  460.5 80.0 %slice-start.5 = ((s8[4718592]{0:T(1024)(128)(4,1)}), s8[4194304]{0:T(1024)(128)(4,1)S(1)}, s32[]{:S(2)}) async-start(s8[4718592]{0:T(1024)(128)(4,1)} %bitcast.87), calls=%async_computation.7 | async-start | bytes 8388608
  540.5 99.7 %copy-start.2 = (s32[16]{0:T(128)S(1)}, s32[16]{0:T(128)}, u32[]{:S(2)}) copy-start(s32[16]{0:T(128)} %param.7) | copy-start | bytes 196
  540.5 99.7 %copy-start.4 = (f32[16,16]{0,1:T(8,128)S(1)}, f32[16,16]{0,1:T(8,128)}, u32[]{:S(2)}) copy-start(f32[16,16]{0,1:T(8,128)} %constant.146) | copy-start | bytes 3076
  540.6 125.4 %copy-start.3 = (f32[16,16]{0,1:T(8,128)S(1)}, f32[16,16]{0,1:T(8,128)}, u32[]{:S(2)}) copy-start(f32[16,16]{0,1:T(8,128)} %constant.147) | copy-start | bytes 3076
  636.7 13.9 %all-to-all-start = ((f32[8,64,288]{2,1,0:T(8,128)}), f32[8,64,288]{2,1,0:T(8,128)S(1)}, u32[]{:S(2)}, u32[]{:S(2)}) async-start(f32[8,64,288]{2,1,0:T(8,128)} %bitcast.7), calls=%async_computation | async-start | bytes 1572864 | tf_op jit(solution)/shard_map/all_to_all | solution.py:22
  651.3 20.6 %all-to-all-start.1 = ((f32[16,4,288]{2,1,0:T(4,128)}), f32[16,4,288]{2,1,0:T(4,128)S(1)}, u32[]{:S(2)}, u32[]{:S(2)}) async-start(f32[16,4,288]{2,1,0:T(4,128)} %reshape.89), calls=%async_computation.1 | async-start | bytes 196608 | tf_op jit(solution)/shard_map/all_to_all | solution.py:22
where the time goes:
time: 684 us; the launch traced here: 679 us
  blocking collectives  311 us (45%)
  matrix products  200 us (29%)
  other arithmetic  82.4 us (12%)
  local copies, waits for them, and re-layouts  51.7 us (8%)
  starting transfers between devices  18.2 us (3%)
  waiting for transfers between devices  15.9 us (2%)
    all_gather x1, blocking collectives, body(): gathered = lax.all_gather(momenta, ('gx', 'gz', 'ta'), axis=0, tiled=True)  311 us
    dot_general x1, matrix products, single_block(): third = jnp.einsum('ms,cs->mc', -sine, summed_part, precision=high)  94.9 us
    dot_general x1, matrix products, single_block(): second = jnp.einsum('ms,cs->mc', cosine, diff_part, precision=high)  80 us
    dot_general x1, other arithmetic, single_block(): first = jnp.einsum('ms,cs->mc', cosine - sine, plain_re, precision=high)  72.3 us
    slice x1, local copies, waits for them, and re-layouts, body(): plain_im = propagator[1].reshape(144, local_sites)  32.7 us
    dot_general x1, matrix products, single_block(): first = jnp.einsum('ms,cs->mc', cosine - sine, plain_re, precision=high)  20.4 us
    all_to_all x2, starting transfers between devices, summed_on_arrival(): lax.all_to_all(in_blocks(array, dim, devices), axis, 0, 0, tiled=True)  18.2 us
    all_to_all x2, waiting for transfers between devices, summed_on_arrival(): lax.all_to_all(in_blocks(array, dim, devices), axis, 0, 0, tiled=True)  15.9 us
  transfers between devices with their start and end apart: 2, of which 2 were waited for; matrix products, arithmetic and copies ran while one was open for 0% of the time, Pallas kernels for 0%

commit v1 on v0

v1 whole, which is shorter than its diff:
```python
import functools
import math

import jax
import jax.numpy as jnp
import numpy as np
from jax import lax
from jax.experimental import pallas as pl
from jax.experimental.pallas import tpu as pltpu
from jax.sharding import PartitionSpec as P

LX = LY = LZ = LT = 32
MESH = pl.DeviceIdType.MESH
F32 = jnp.float32
BF16 = jnp.bfloat16
TILES = 11
CHUNKS = 9
ROWS = 384


def fold_matrices():
    out = np.zeros((8, 2, 8, 8, 8, 2))
    for q in range(8):
        r = 2 * q if q < 4 else 2 * (q - 4) + 1
        for h in range(8):
            w = np.exp(-2j * np.pi * r * h / 8)
            for x in range(8):
                out[q, 0, x, x, h, 0] = w.real
                out[q, 0, x, x, h, 1] = -w.imag
                out[q, 1, x, x, h, 0] = w.imag
                out[q, 1, x, x, h, 1] = w.real
    full = out.reshape(128, 128).astype(np.float32)
    high = full.astype(jnp.bfloat16)
    low = (full - high.astype(np.float32)).astype(jnp.bfloat16)
    return np.concatenate([high, high], 1), np.concatenate([low, 0 * low], 1)[64:]


def split(value):
    high = value.astype(BF16)
    return high, (value - high.astype(F32)).astype(BF16)


def sine(index):
    turn = ((index + 16) & 31) - 16
    turn = jnp.where(turn > 8, 16 - turn, jnp.where(turn < -8, -16 - turn, turn))
    u = turn.astype(F32) * (math.pi / 16)
    s = u * u
    poly = 1 / 362880 - s * (1 / 39916800)
    for factor in (-1 / 5040, 1 / 120, -1 / 6, 1.0):
        poly = factor + s * poly
    return u * poly


def wave(index):
    return sine(index + 8), -sine(index)


def sum_over_x(value):
    groups = value.shape[0] // 8
    value = value.reshape(groups, 8, 8, 128)
    sub = lax.broadcasted_iota(jnp.int32, (8, 128), 0)
    for step in (4, 2, 1):
        keep = (sub & step) == 0
        out = []
        for k in range(step):
            a, b = value[:, k], value[:, k + step]
            rolled_a = pltpu.roll(a, 8 - step, 1)
            rolled_b = pltpu.roll(b, step, 1)
            out.append(jnp.where(keep, a, rolled_b) + jnp.where(keep, rolled_a, b))
        value = jnp.stack(out, axis=1)
    return value.reshape(groups * 8, 128)


NT = (((1,), (1,)), ((), ()))


def iota(shape, dim):
    return lax.broadcasted_iota(jnp.int32, shape, dim)


def compute_kernel(
    row_order, x_hbm, mom_ref, fold_ref, fold_low_ref, z_ref, sbuf, gh, gl, yall, pick, sems
):
    copies = []
    for k in range(CHUNKS):
        part = pl.ds(k * 16, 16)
        copies.append(pltpu.make_async_copy(x_hbm.at[part], sbuf.at[part], sems.at[k]))
        copies[-1].start()
    gx, gz, ta = (lax.axis_index(name) for name in ("gx", "gz", "ta"))

    for k in range(CHUNKS):
        copies[k].wait()

        def pair_step(p, carry, k=k):
            pair = k * 8 + p
            both = jnp.concatenate([sbuf[2 * pair], sbuf[2 * pair + 1]], axis=1)
            weights = jnp.concatenate(split(both), axis=0)
            out = jnp.dot(fold_ref[...], weights, preferred_element_type=F32)
            low = jnp.dot(fold_low_ref[...], weights, preferred_element_type=F32)
            out = jnp.concatenate([out[:64], out[64:] + low], axis=0)
            left = out[:, :128].reshape(16, 8, 128)
            right = out[:, 128:].reshape(16, 8, 128)
            high, rest = split(jnp.concatenate([left, right], axis=1))
            rows = pl.ds(pl.multiple_of(pair * 16, 16), 16)
            for q in range(8):
                for part in range(2):
                    lanes = slice(part * 128, part * 128 + 128)
                    gh[q, rows, lanes] = high[2 * q + part]
                    gl[q, rows, lanes] = rest[2 * q + part]
            return carry

        lax.fori_loop(0, 8, pair_step, 0)

    turned = jnp.transpose((mom_ref[...] & 31).astype(F32))
    mom = jnp.concatenate([turned[4 * i : 4 * i + 4] for i in range(4)], axis=1)
    ny = mom[1:2].astype(jnp.int32)
    cls = ((ny >> 1) & 3) + 4 * (ny & 1)
    member = (iota((8, 512), 0) == cls).astype(F32)
    before = (iota((512, 512), 0) < iota((512, 512), 1)).astype(F32).astype(BF16)
    ahead = jnp.dot(member.astype(BF16), before, preferred_element_type=F32)
    slot = jnp.sum(member * ahead, axis=0, keepdims=True)
    ends = []
    start = jnp.int32(0)
    for q in range(8):
        count = jnp.sum(member[q : q + 1]).astype(jnp.int32)
        slot = slot + member[q : q + 1] * (start * 128).astype(F32)
        start = start + ((count + 127) >> 7)
        ends.append(start)
    slot = slot.astype(jnp.int32)
    mom8 = jnp.concatenate([mom, jnp.zeros_like(mom)], axis=0).astype(BF16)
    digits = jnp.concatenate([slot >> 5, slot & 31] + [slot * 0] * 6, axis=0).astype(F32).astype(BF16)
    source = row_order(iota((512, 512), 0))
    move = (source == iota((512, 512), 1)).astype(F32).astype(BF16)
    column = lax.dot_general(move, digits, NT, preferred_element_type=F32)
    column = (column[:, 0:1] * 32.0 + column[:, 1:2]).astype(jnp.int32)

    def tile_step(j, carry):
        q = jnp.int32(0)
        for end in ends[:7]:
            q = q + (end <= j).astype(jnp.int32)
        here = (iota((128, 512), 0) + j * 128 == slot).astype(F32).astype(BF16)
        sorted_mom = lax.dot_general(mom8, here, NT, preferred_element_type=F32).astype(jnp.int32)
        nx, ny, nz, nt = (sorted_mom[i : i + 1] for i in range(4))
        site = iota((128, 128), 0)
        pr, pi = wave(ny * (site >> 5) + nz * ((site >> 2) & 7) + nt * (site & 3))
        (prh, prl), (pih, pil) = split(pr), split(pi)
        w_high = jnp.concatenate(
            [jnp.concatenate([prh, pih], 1), jnp.concatenate([-pih, prh], 1)], 0
        )
        w_low = jnp.concatenate(
            [jnp.concatenate([prl, pil], 1), jnp.concatenate([-pil, prl], 1)], 0
        )
        xr, xi = wave(nx * (gx * 8 + iota((8, 128), 0)) + nz * (gz * 8) + nt * (ta * 4))
        lanes = pl.ds(pl.multiple_of(j * 256, 256), 128)
        lanes_low = pl.ds(pl.multiple_of(j * 256 + 128, 128), 128)
        for c in range(1152 // ROWS):
            rows = pl.ds(c * ROWS, ROWS)
            high = gh[q, rows]
            out = (
                jnp.dot(high, w_high, preferred_element_type=F32)
                + jnp.dot(gl[q, rows], w_high, preferred_element_type=F32)
                + jnp.dot(high, w_low, preferred_element_type=F32)
            )
            re = out[:, :128].reshape(ROWS // 8, 8, 128)
            im = out[:, 128:].reshape(ROWS // 8, 8, 128)
            for part, value in enumerate((re * xr - im * xi, re * xi + im * xr)):
                top, rest = split(sum_over_x(value))
                to = pl.ds(part * 144 + c * (ROWS // 8), ROWS // 8)
                yall[to, lanes] = top
                yall[to, lanes_low] = rest
        chosen = (iota((512, 128), 1) + j * 128 == column).astype(F32).astype(BF16)
        pick[:, lanes] = chosen
        pick[:, lanes_low] = chosen
        return carry

    lax.fori_loop(0, TILES, tile_step, 0)
    z_ref[...] = lax.dot_general(pick[...], yall[...], NT, preferred_element_type=F32)


def partial_spectrum(x, mom, row_order):
    fold, fold_low = fold_matrices()
    vmem = pl.BlockSpec(memory_space=pltpu.VMEM)
    return pl.pallas_call(
        functools.partial(compute_kernel, row_order),
        out_shape=jax.ShapeDtypeStruct((512, 288), F32),
        in_specs=[pl.BlockSpec(memory_space=pl.ANY), vmem, vmem, vmem],
        out_specs=vmem,
        scratch_shapes=[
            pltpu.VMEM((144, 128, 128), F32),
            pltpu.VMEM((8, 1152, 256), BF16),
            pltpu.VMEM((8, 1152, 256), BF16),
            pltpu.VMEM((288, TILES * 256), BF16),
            pltpu.VMEM((512, TILES * 256), BF16),
            pltpu.SemaphoreType.DMA((CHUNKS,)),
        ],
        compiler_params=pltpu.CompilerParams(vmem_limit_bytes=50 * 1024 * 1024),
    )(x, mom, jnp.asarray(fold), jnp.asarray(fold_low))


def gather_kernel(sizes, row_ref, out_ref, send_sem, recv_sem):
    n_gx, n_gz, n_ta = sizes
    total = n_gx * n_gz * n_ta
    me = (lax.axis_index("gx") * n_gz + lax.axis_index("gz")) * n_ta + lax.axis_index("ta")

    def device(k):
        peer = lax.rem(me + k, total)
        return (peer // (n_gz * n_ta), lax.rem(peer // n_ta, n_gz), lax.rem(peer, n_ta))

    barrier = pltpu.get_barrier_semaphore()

    def greet(k, carry):
        pl.semaphore_signal(barrier, inc=1, device_id=device(k), device_id_type=MESH)
        return carry

    lax.fori_loop(1, total, greet, 0)
    out_ref[me] = row_ref[...]
    pl.semaphore_wait(barrier, total - 1)

    def copy(k):
        return pltpu.make_async_remote_copy(
            src_ref=row_ref,
            dst_ref=out_ref.at[me],
            send_sem=send_sem,
            recv_sem=recv_sem,
            device_id=device(k),
            device_id_type=MESH,
        )

    def send(k, carry):
        copy(k).start()
        return carry

    lax.fori_loop(1, total, send, 0)
    everything = out_ref.at[pl.ds(0, total - 1)]
    pltpu.make_async_copy(everything, everything, send_sem).wait()
    pltpu.make_async_copy(everything, everything, recv_sem).wait()


def gather_momenta(momenta, sizes):
    total = math.prod(sizes)
    row = jnp.pad(momenta.reshape(1, 16), ((0, 0), (0, 112)))
    vmem = pl.BlockSpec(memory_space=pltpu.VMEM)
    out = pl.pallas_call(
        functools.partial(gather_kernel, sizes),
        out_shape=jax.ShapeDtypeStruct((total, 1, 128), jnp.int32),
        in_specs=[vmem],
        out_specs=vmem,
        scratch_shapes=[pltpu.SemaphoreType.DMA, pltpu.SemaphoreType.DMA],
        compiler_params=pltpu.CompilerParams(collective_id=0, has_side_effects=True),
    )(row)
    return out.reshape(total, 128)


def in_blocks(array, dim, devices):
    before, after = (array.shape[:dim], array.shape[dim + 1 :])
    return jnp.moveaxis(array.reshape(*before, devices, -1, *after), dim, 0)


def summed_on_arrival(array, axis, dim):
    devices = lax.axis_size(axis)
    blocks = lax.all_to_all(in_blocks(array, dim, devices), axis, 0, 0, tiled=True)
    return jnp.sum(blocks, axis=0)


def clifford_table():
    zeros = np.zeros((4, 4))
    first = (zeros, np.array([[0, 0, 0, 1], [0, 0, 1, 0], [0, -1, 0, 0], [-1, 0, 0, 0]]))
    second = (np.array([[0, 0, 0, -1], [0, 0, 1, 0], [0, 1, 0, 0], [-1, 0, 0, 0]]), zeros)
    third = (zeros, np.array([[0, 0, 1, 0], [0, 0, 0, -1], [-1, 0, 0, 0], [0, 1, 0, 0]]))
    fourth = (np.array([[0, 0, 1, 0], [0, 0, 0, 1], [1, 0, 0, 0], [0, 1, 0, 0]]), zeros)
    basis = [first, second, third, fourth]
    tables_re = []
    tables_im = []
    for mask in range(16):
        matrix_re = np.identity(4)
        matrix_im = np.zeros((4, 4))
        for bit in range(4):
            if mask >> bit & 1:
                basis_re, basis_im = basis[bit]
                new_re = matrix_re @ basis_re - matrix_im @ basis_im
                new_im = matrix_re @ basis_im + matrix_im @ basis_re
                matrix_re, matrix_im = (new_re, new_im)
        tables_re.append(matrix_re)
        tables_im.append(matrix_im)
    return (np.stack(tables_re), np.stack(tables_im))


def select_gammas(gamma_index):
    table_re, table_im = clifford_table()
    onehot = (gamma_index[:, None] == jnp.arange(16, dtype=jnp.int32)[None, :]).astype(jnp.float32)
    high = lax.Precision.HIGHEST
    chosen_re = jnp.einsum(
        "gk,kst->gst", onehot, jnp.asarray(table_re, jnp.float32), precision=high
    )
    chosen_im = jnp.einsum(
        "gk,kst->gst", onehot, jnp.asarray(table_im, jnp.float32), precision=high
    )
    return (chosen_re, chosen_im)


def vertices_of(spec_re, spec_im, gamma_re, gamma_im):
    high = lax.Precision.HIGHEST
    count = spec_re.shape[0]
    split_re = spec_re.reshape(count, 4, 3, 12)
    split_im = spec_im.reshape(count, 4, 3, 12)
    turned_re = (
        jnp.einsum("gst,mtcb->mgscb", gamma_re, split_re, precision=high)
        - jnp.einsum("gst,mtcb->mgscb", gamma_im, split_im, precision=high)
    ).reshape(count, 16, 12, 12)
    turned_im = (
        jnp.einsum("gst,mtcb->mgscb", gamma_re, split_im, precision=high)
        + jnp.einsum("gst,mtcb->mgscb", gamma_im, split_re, precision=high)
    ).reshape(count, 16, 12, 12)
    result_re = jnp.einsum("mka,mgkb->mgab", spec_re, turned_re, precision=high) + jnp.einsum(
        "mka,mgkb->mgab", spec_im, turned_im, precision=high
    )
    result_im = jnp.einsum("mka,mgkb->mgab", spec_re, turned_im, precision=high) - jnp.einsum(
        "mka,mgkb->mgab", spec_im, turned_re, precision=high
    )
    return jnp.stack([result_re, result_im], axis=2)


def site_major(propagator):
    x = jnp.transpose(propagator, (1, 2, 0, 3)).reshape(144, 2, 64, 128)
    return jnp.transpose(x, (0, 2, 1, 3)).reshape(144, 128, 128)


def body(sizes, propagator, momenta, gamma_index):
    mine = momenta.shape[0]
    total = math.prod(sizes)
    n_ta = sizes[2]
    gathered = gather_momenta(momenta, sizes)

    def row_order(row):
        ta, spatial, own = row // (total // n_ta * mine), row // mine % (total // n_ta), row % mine
        return own * total + spatial * n_ta + ta

    partial_value = partial_spectrum(site_major(propagator), gathered, row_order)
    partial_value = summed_on_arrival(partial_value, "ta", 0)
    spectrum = summed_on_arrival(partial_value, ("gx", "gz"), 0)
    spectrum = spectrum * (1.0 / math.sqrt(float(LX * LY * LZ * LT)))
    spectrum = spectrum.reshape(mine, 2, 12, 12)
    gamma_re, gamma_im = select_gammas(gamma_index)
    return vertices_of(spectrum[:, 0], spectrum[:, 1], gamma_re, gamma_im)


def solution(mesh):
    placed = (P(None, None, None, ("gx", "gz", "ta")), P(("gx", "gz", "ta"), None), P())
    sizes = tuple(mesh.shape[name] for name in ("gx", "gz", "ta"))
    return jax.shard_map(
        functools.partial(body, sizes),
        mesh=mesh,
        in_specs=placed,
        out_specs=P(("gx", "gz", "ta"), None, None, None, None),
        check_vma=False,
    )
```

time: 684 us -> 90.9 us (0.13)
  blocking collectives: 311 us -> 0 us
  matrix products: 200 us -> 4.47 us
  other arithmetic: 82.4 us -> 0.15 us
  Pallas kernels: 0 us -> 48.7 us
  local copies, waits for them, and re-layouts: 51.7 us -> 7.13 us
  starting transfers between devices: 18.2 us -> 10.9 us
    all_gather x1 -> x0, blocking collectives: 311 us -> none  [body(): gathered = lax.all_gather(momenta, ('gx', 'gz', 'ta'), axis=0, tiled=True)]
    dot_general x3 -> x0, matrix products: 195 us -> none  [the longest x1 94.9 us: single_block(): third = jnp.einsum('ms,cs->mc', -sine, summed_part, precision=high)]
    dot_general x3 -> x0, other arithmetic: 82.1 us -> none  [the longest x1 72.3 us: single_block(): first = jnp.einsum('ms,cs->mc', cosine - sine, plain_re, precision=high)]
    pallas_call x0 -> x2, Pallas kernels: none -> 48.7 us  [the longest x1 30.1 us: partial_spectrum(): pl.pallas_call(functools.partial(compute_kernel, row_order), out_shape=ja...]
    slice x1 -> x0, local copies, waits for them, and re-layouts: 32.7 us -> none  [body(): plain_im = propagator[1].reshape(144, local_sites)]
    another operation x2 -> x0, local copies, waits for them, and re-layouts: 12 us -> none  [the longest x1 6 us: body(): plain_im = propagator[1].reshape(144, local_sites)]
    all_to_all x2, starting transfers between devices: 18.2 us -> 10.9 us  [summed_on_arrival(): lax.all_to_all(in_blocks(array, dim, devices), axis, 0, 0, tiled=True)]
where the time goes in v1:
time: 90.9 us; the launch traced here: 90.5 us
  Pallas kernels  48.7 us (54%)
  waiting for transfers between devices  18.9 us (21%)
  starting transfers between devices  10.9 us (12%)
  local copies, waits for them, and re-layouts  7.13 us (8%)
  matrix products  4.47 us (5%)
    pallas_call x1, Pallas kernels, partial_spectrum(): pl.pallas_call(functools.partial(compute_kernel, row_order), out_shape=ja...  30.1 us
    all_to_all x2, waiting for transfers between devices, summed_on_arrival(): lax.all_to_all(in_blocks(array, dim, devices), axis, 0, 0, tiled=True)  18.9 us
    pallas_call x1, Pallas kernels, gather_momenta(): pl.pallas_call(functools.partial(gather_kernel, sizes), out_shape=jax.Sha...  18.6 us
    all_to_all x2, starting transfers between devices, summed_on_arrival(): lax.all_to_all(in_blocks(array, dim, devices), axis, 0, 0, tiled=True)  10.9 us
    unnamed x13, local copies, waits for them, and re-layouts  2.45 us
  transfers between devices with their start and end apart: 2, of which 2 were waited for; matrix products, arithmetic and copies ran while one was open for 0% of the time, Pallas kernels for 0%

profile of v1, /device:TPU:1, one launch (start us, length us, event | category | flops | bytes accessed | tf_op | source)
XLA Modules:
  0.0 90.5 jit_solution(16625556841139804451)
XLA Ops:
  0.0 0.8 reshape.31
  0.8 0.5 pad.4.row_ref
  1.3 18.6 %shard_map.73 = s32[128,1,128]{2,1,0:T(1,128)} custom-call(s32[1,128]{1,0:T(1,128)} %pad.4.row_ref), custom_call_target="tpu_custom_call" | custom-call | tf_op jit(solution)/shard_map/pallas_call | solution.py:243
  20.0 0.0 copy-start
  20.0 0.8 copy-done
  20.8 0.8 copy-done.1
  21.7 0.8 copy-done.2
  22.4 30.1 %shard_map.74 = f32[512,288]{1,0:T(8,128)} custom-call(f32[144,128,128]{2,1,0:T(8,128)} %bitcast.76, s32[128,128]{1,0:T(8,128)S(1)} %bitcast.75, bf16[128,256]{1,0:T(8,128)(2,1)S(1)} %copy-done.1, bf16[64,256]{1,0:T(8,128)(2,1)S(1)} %copy-done.2), custom_call_target="tpu_custom_call" | custom-call | tf_op jit(solution)/shard_map/pallas_call | solution.py:183
  52.5 5.3 %all-to-all-start = ((f32[8,64,288]{2,1,0:T(8,128)}), f32[8,64,288]{2,1,0:T(8,128)S(1)}, u32[]{:S(2)}, u32[]{:S(2)}) async-start(f32[8,64,288]{2,1,0:T(8,128)} %bitcast.5), calls=%async_computation | async-start | bytes 1572864 | tf_op jit(solution)/shard_map/all_to_all | solution.py:261
  57.8 0.0 copy-done.5
  57.8 0.0 copy-done.3
  57.8 0.2 fusion.21
  58.0 13.2 %all-to-all-done = f32[8,64,288]{2,1,0:T(8,128)S(1)} async-done(((f32[8,64,288]{2,1,0:T(8,128)}), f32[8,64,288]{2,1,0:T(8,128)S(1)}, u32[]{:S(2)}, u32[]{:S(2)}) %all-to-all-start) | async-done | bytes 589856 | tf_op jit(solution)/shard_map/all_to_all | solution.py:261
  71.3 0.7 reshape.34
  72.0 5.6 %all-to-all-start.1 = ((f32[16,4,288]{2,1,0:T(4,128)}), f32[16,4,288]{2,1,0:T(4,128)S(1)}, u32[]{:S(2)}, u32[]{:S(2)}) async-start(f32[16,4,288]{2,1,0:T(4,128)} %reshape.34), calls=%async_computation.1 | async-start | bytes 196608 | tf_op jit(solution)/shard_map/all_to_all | solution.py:261
  77.6 0.2 fusion.20
  77.7 5.7 %all-to-all-done.1 = f32[16,4,288]{2,1,0:T(4,128)S(1)} async-done(((f32[16,4,288]{2,1,0:T(4,128)}), f32[16,4,288]{2,1,0:T(4,128)S(1)}, u32[]{:S(2)}, u32[]{:S(2)}) %all-to-all-start.1) | async-done | bytes 73760 | tf_op jit(solution)/shard_map/all_to_all | solution.py:261
  83.5 0.1 mul.12
  83.7 0.6 fusion.14
  84.2 0.6 fusion.18
  84.8 0.6 fusion.2
  85.4 0.2 copy.54
  85.6 0.4 copy.55
  85.9 0.6 fusion.3
  86.5 0.2 copy.50
  86.7 0.4 copy.51
  87.1 0.5 fusion.8
  87.5 0.5 fusion.6
  88.0 0.5 fusion.1
  88.5 0.5 fusion
  88.9 0.1 pad_maximum_fusion
  89.0 1.5 %copy.58 = f32[4,16,2,12,12]{1,2,4,3,0:T(2,128)} copy(f32[4,16,2,12,12]{3,1,4,0,2:T(8,128)S(1)} %pad_maximum_fusion) | data formatting | bytes 147456 | tf_op jit(solution)/shard_map/stack | solution.py:320
  (12 shorter events, 0.1 us)
Async XLA Ops:
  0.0 57.8 %copy-start.5 = (f32[16,16]{0,1:T(8,128)S(1)}, f32[16,16]{0,1:T(8,128)}, u32[]{:S(2)}) copy-start(f32[16,16]{0,1:T(8,128)} %constant.21) | copy-start | bytes 3076
  0.0 77.6 %copy-start.4 = (f32[16,16]{0,1:T(8,128)S(1)}, f32[16,16]{0,1:T(8,128)}, u32[]{:S(2)}) copy-start(f32[16,16]{0,1:T(8,128)} %constant.22) | copy-start | bytes 3076
  0.0 57.8 %copy-start.3 = (s32[16]{0:T(128)S(1)}, s32[16]{0:T(128)}, u32[]{:S(2)}) copy-start(s32[16]{0:T(128)} %param.9) | copy-start | bytes 196
  20.0 0.8 copy-start
  20.8 0.8 copy-start.1
  21.6 0.8 copy-start.2
  52.5 18.8 %all-to-all-start = ((f32[8,64,288]{2,1,0:T(8,128)}), f32[8,64,288]{2,1,0:T(8,128)S(1)}, u32[]{:S(2)}, u32[]{:S(2)}) async-start(f32[8,64,288]{2,1,0:T(8,128)} %bitcast.5), calls=%async_computation | async-start | bytes 1572864 | tf_op jit(solution)/shard_map/all_to_all | solution.py:261
  72.0 11.5 %all-to-all-start.1 = ((f32[16,4,288]{2,1,0:T(4,128)}), f32[16,4,288]{2,1,0:T(4,128)S(1)}, u32[]{:S(2)}, u32[]{:S(2)}) async-start(f32[16,4,288]{2,1,0:T(4,128)} %reshape.34), calls=%async_computation.1 | async-start | bytes 196608 | tf_op jit(solution)/shard_map/all_to_all | solution.py:261

commit v2 on v1

v2 whole, which is shorter than its diff:
```python
import math

import jax
import jax.numpy as jnp
import numpy as np
from jax import lax
from jax.experimental import pallas as pl
from jax.experimental.pallas import tpu as pltpu
from jax.sharding import PartitionSpec as P

LX = LY = LZ = LT = 32
MESH = pl.DeviceIdType.MESH
F32 = jnp.float32
BF16 = jnp.bfloat16
TILES = 11
CHUNKS = 18
HALF = 72


def split(value):
    high = value.astype(BF16)
    return high, (value - high.astype(F32)).astype(BF16)


def sine(index):
    turn = ((index + 16) & 31) - 16
    turn = jnp.where(turn > 8, 16 - turn, jnp.where(turn < -8, -16 - turn, turn))
    u = turn.astype(F32) * (math.pi / 16)
    s = u * u
    poly = 1 / 362880 - s * (1 / 39916800)
    for factor in (-1 / 5040, 1 / 120, -1 / 6, 1.0):
        poly = factor + s * poly
    return u * poly


def wave(index):
    return sine(index + 8), -sine(index)


def sum_over_x(value):
    groups = value.shape[0] // 8
    value = value.reshape(groups, 8, 8, 128)
    sub = lax.broadcasted_iota(jnp.int32, (8, 128), 0)
    for step in (4, 2, 1):
        keep = (sub & step) == 0
        out = []
        for k in range(step):
            a, b = value[:, k], value[:, k + step]
            rolled_a = pltpu.roll(a, 8 - step, 1)
            rolled_b = pltpu.roll(b, step, 1)
            out.append(jnp.where(keep, a, rolled_b) + jnp.where(keep, rolled_a, b))
        value = jnp.stack(out, axis=1)
    return value.reshape(groups * 8, 128)


NT = (((1,), (1,)), ((), ()))


def iota(shape, dim):
    return lax.broadcasted_iota(jnp.int32, shape, dim)


def fold_matrix():
    row, col = iota((128, 128), 0), iota((128, 128), 1)
    q = row >> 4
    number = jnp.where(q < 4, 2 * q, 2 * q - 7)
    re, im = wave(4 * number * ((col >> 1) & 7))
    from_im, to_im = (col & 1) == 1, ((row >> 3) & 1) == 1
    value = jnp.where(from_im == to_im, re, jnp.where(to_im, im, -im))
    return split(jnp.where((row & 7) == (col >> 4), value, 0.0))


def program_kernel(
    x_hbm, mom_smem, out_ref,
    sbuf, gh, gl, w_high, w_low, x_wave, yall, pick, row_buf, mom_all,
    zbuf, dbuf, hbuf, rbuf, spec,
    in_sems, mom_send, mom_recv, pair_send, pair_recv, far_send, far_recv, last_send, last_recv,
):
    gx, gz, ta = (lax.axis_index(name) for name in ("gx", "gz", "ta"))
    core, y_lo, z, y_hi = gz % 2, gz // 2, ta // 2, ta % 2
    y = y_hi * 2 + y_lo
    me = (gx * 4 + gz) * 8 + ta
    chip = (gx * 2 + y_lo) * 8 + ta
    xs = [gx] + [(gx + k) % 4 for k in range(1, 4)]
    ys = [y] + [(y + k) % 4 for k in range(1, 4)]
    zs = [z] + [(z + k) % 4 for k in range(1, 4)]
    cores = [core, 1 - core]
    gzs = [[(value % 2) * 2 + c for c in cores] for value in ys]
    tas = [[at_z * 2 + value // 2 for at_z in zs] for value in ys]
    hops = (0, 1, 2, 1)
    chips = sorted(
        ((dx, dy, dz) for dx in range(4) for dy in range(4) for dz in range(4)),
        key=lambda d: -sum(hops[k] for k in d),
    )

    def device(place, dc=0):
        dx, dy, dz = place
        return (xs[dx], gzs[dy][dc], tas[dy][dz])

    def chip_of(place):
        dx, dy, dz = place
        return (xs[dx] * 2 + ys[dy] % 2) * 8 + tas[dy][dz]

    others = [(place, dc) for place in chips for dc in (0, 1) if place != (0, 0, 0) or dc]
    barrier = pltpu.get_barrier_semaphore()
    for place, dc in others:
        pl.semaphore_signal(barrier, inc=1, device_id=device(place, dc), device_id_type=MESH)

    def load(k):
        part = pl.ds(k * 8, 8)
        return pltpu.make_async_copy(x_hbm.at[part], sbuf.at[part], in_sems.at[k])

    for k in range(CHUNKS):
        load(k).start()
    row = jnp.zeros((1, 128), jnp.int32)
    for i in range(4):
        for k in range(4):
            row = jnp.where(iota((1, 128), 1) == 4 * i + k, mom_smem[i, k], row)
    row_buf[...] = row
    mom_all[me] = row

    fold_high, fold_low = fold_matrix()
    fold_twice = jnp.concatenate([fold_high, fold_high], axis=1)
    fold_rest = jnp.concatenate([fold_low, jnp.zeros_like(fold_low)], axis=1)[64:]

    def fold_step(k, carry):
        load(k).wait()
        for p in range(4):
            pair = k * 4 + p
            both = jnp.concatenate([sbuf[2 * pair], sbuf[2 * pair + 1]], axis=1)
            weights = jnp.concatenate(split(both), axis=0)
            out = jnp.dot(fold_twice, weights, preferred_element_type=F32)
            low = jnp.dot(fold_rest, weights, preferred_element_type=F32)
            out = jnp.concatenate([out[:64], out[64:] + low], axis=0)
            left = out[:, :128].reshape(16, 8, 128)
            right = out[:, 128:].reshape(16, 8, 128)
            high, rest = split(jnp.concatenate([left, right], axis=1))
            rows = pl.ds(pl.multiple_of(pair * 16, 16), 16)
            for q in range(8):
                for part in range(2):
                    lanes = slice(part * 128, part * 128 + 128)
                    gh[q, rows, lanes] = high[2 * q + part]
                    gl[q, rows, lanes] = rest[2 * q + part]
        return carry

    lax.fori_loop(0, CHUNKS // 2, fold_step, 0)

    pl.semaphore_wait(barrier, 127)
    for place, dc in others:
        pltpu.make_async_remote_copy(
            src_ref=row_buf, dst_ref=mom_all.at[me], send_sem=mom_send, recv_sem=mom_recv,
            device_id=device(place, dc), device_id_type=MESH,
        ).start()

    lax.fori_loop(CHUNKS // 2, CHUNKS, fold_step, 0)

    all_rows = mom_all.at[pl.ds(0, 127)]
    pltpu.make_async_copy(all_rows, all_rows, mom_recv).wait()

    turned = jnp.transpose((mom_all[...].reshape(128, 128) & 31).astype(F32))
    mom = jnp.concatenate([turned[4 * i : 4 * i + 4] for i in range(4)], axis=1)
    ny = mom[1:2].astype(jnp.int32)
    cls = ((ny >> 1) & 3) + 4 * (ny & 1)
    member = (iota((8, 512), 0) == cls).astype(F32)
    before = (iota((512, 512), 0) < iota((512, 512), 1)).astype(F32).astype(BF16)
    ahead = jnp.dot(member.astype(BF16), before, preferred_element_type=F32)
    slot = jnp.sum(member * ahead, axis=0, keepdims=True)
    ends = []
    start = jnp.int32(0)
    for q in range(8):
        count = jnp.sum(member[q : q + 1]).astype(jnp.int32)
        slot = slot + member[q : q + 1] * (start * 128).astype(F32)
        start = start + ((count + 127) >> 7)
        ends.append(start)
    slot = slot.astype(jnp.int32)
    mom8 = jnp.concatenate([mom, jnp.zeros_like(mom)], axis=0).astype(BF16)
    digits = jnp.concatenate([slot >> 5, slot & 31] + [slot * 0] * 6, axis=0).astype(F32).astype(BF16)
    to_row = iota((512, 512), 0)
    to_chip, to_core, own = to_row >> 3, (to_row >> 2) & 1, to_row & 3
    source = own * 128 + ((to_chip >> 3) * 2 + to_core) * 8 + (to_chip & 7)
    move = (source == iota((512, 512), 1)).astype(F32).astype(BF16)
    column = lax.dot_general(move, digits, NT, preferred_element_type=F32)
    column = (column[:, 0:1] * 32.0 + column[:, 1:2]).astype(jnp.int32)

    def prepare(j):
        here = (iota((128, 512), 0) + j * 128 == slot).astype(F32).astype(BF16)
        sorted_mom = lax.dot_general(mom8, here, NT, preferred_element_type=F32).astype(jnp.int32)
        nx, ny, nz, nt = (sorted_mom[i : i + 1] for i in range(4))
        site = iota((128, 128), 0)
        pr, pi = wave(ny * (site >> 5) + nz * ((site >> 2) & 7) + nt * (site & 3))
        (prh, prl), (pih, pil) = split(pr), split(pi)
        w_high[j] = jnp.concatenate(
            [jnp.concatenate([prh, pih], 1), jnp.concatenate([-pih, prh], 1)], 0
        )
        w_low[j] = jnp.concatenate(
            [jnp.concatenate([prl, pil], 1), jnp.concatenate([-pil, prl], 1)], 0
        )
        xr, xi = wave(nx * (gx * 8 + iota((8, 128), 0)) + nz * (gz * 8) + nt * (ta * 4))
        x_wave[j, 0] = xr
        x_wave[j, 1] = xi

    def multiply(j, half):
        q = jnp.int32(0)
        for end in ends[:7]:
            q = q + (end <= j).astype(jnp.int32)
        rows = pl.ds(half * HALF * 8, HALF * 8)
        high = gh[q, rows]
        top = w_high[j]
        out = (
            jnp.dot(high, top, preferred_element_type=F32)
            + jnp.dot(gl[q, rows], top, preferred_element_type=F32)
            + jnp.dot(high, w_low[j], preferred_element_type=F32)
        )
        xr, xi = x_wave[j, 0], x_wave[j, 1]
        re = out[:, :128].reshape(HALF, 8, 128)
        im = out[:, 128:].reshape(HALF, 8, 128)
        lanes = pl.ds(pl.multiple_of(j * 256, 256), 128)
        lanes_low = pl.ds(pl.multiple_of(j * 256 + 128, 128), 128)
        for part, value in enumerate((re * xr - im * xi, re * xi + im * xr)):
            first, rest = split(sum_over_x(value))
            to = pl.ds(part * 128, HALF)
            yall[half, to, lanes] = first
            yall[half, to, lanes_low] = rest

    def choose(j):
        lanes = pl.ds(pl.multiple_of(j * 256, 256), 128)
        lanes_low = pl.ds(pl.multiple_of(j * 256 + 128, 128), 128)
        chosen = (iota((512, 128), 1) + j * 128 == column).astype(F32).astype(BF16)
        pick[:, lanes] = chosen
        pick[:, lanes_low] = chosen

    def first_step(j, carry):
        multiply(j, 0)
        prepare(j + 1)
        choose(j)
        return carry

    def second_step(j, carry):
        multiply(j, 1)
        return carry

    def to_partner(half):
        return pltpu.make_async_remote_copy(
            src_ref=zbuf.at[half, 1 - core], dst_ref=dbuf.at[half],
            send_sem=pair_send.at[half], recv_sem=pair_recv.at[half],
            device_id=device((0, 0, 0), 1), device_id_type=MESH,
        )

    def restore(half):
        back = lax.dot_general(pick[...], yall[half], NT, preferred_element_type=F32)
        zbuf[half, 0] = back[:, :128]
        zbuf[half, 1] = back[:, 128:]
        to_partner(half).start()

    def send_far(half):
        to_partner(half).wait_recv()
        total = (zbuf[half, core] + dbuf[half]) * (1.0 / math.sqrt(float(LX * LY * LZ * LT)))
        hbuf[half] = total.reshape(64, 8, 128)
        rbuf[half, chip] = hbuf[half, chip]
        for place in chips[:-1]:
            pltpu.make_async_remote_copy(
                src_ref=hbuf.at[half, chip_of(place)], dst_ref=rbuf.at[half, chip],
                send_sem=far_send.at[half], recv_sem=far_recv.at[half],
                device_id=device(place), device_id_type=MESH,
            ).start()

    def wait_far(half):
        blocks = rbuf.at[half, pl.ds(0, 63)]
        pltpu.make_async_copy(blocks, blocks, far_recv.at[half]).wait()
        spec[core, half] = jnp.sum(rbuf[half], axis=0)

    prepare(jnp.int32(0))
    lax.fori_loop(0, TILES, first_step, 0)
    restore(0)
    lax.fori_loop(0, TILES // 2, second_step, 0)
    send_far(0)
    lax.fori_loop(TILES // 2, TILES, second_step, 0)
    restore(1)
    send_far(1)
    wait_far(0)
    wait_far(1)
    last = pltpu.make_async_remote_copy(
        src_ref=spec.at[core], dst_ref=spec.at[core], send_sem=last_send, recv_sem=last_recv,
        device_id=device((0, 0, 0), 1), device_id_type=MESH,
    )
    last.start()
    pltpu.make_async_copy(all_rows, all_rows, mom_send).wait()
    for half in range(2):
        to_partner(half).wait_send()
        blocks = hbuf.at[half, pl.ds(0, 63)]
        pltpu.make_async_copy(blocks, blocks, far_send.at[half]).wait()
    last.wait()
    value = spec[...]
    out_ref[...] = jnp.where(core == 0, value[:, :, :4], value[:, :, 4:])


def spectrum_of(x, momenta):
    vmem = pl.BlockSpec(memory_space=pltpu.VMEM)
    dma = pltpu.SemaphoreType.DMA
    return pl.pallas_call(
        program_kernel,
        out_shape=jax.ShapeDtypeStruct((2, 2, 4, 128), F32),
        in_specs=[pl.BlockSpec(memory_space=pl.ANY), pl.BlockSpec(memory_space=pltpu.SMEM)],
        out_specs=vmem,
        scratch_shapes=[
            pltpu.VMEM((144, 128, 128), F32),
            pltpu.VMEM((8, 1152, 256), BF16),
            pltpu.VMEM((8, 1152, 256), BF16),
            pltpu.VMEM((TILES + 1, 256, 256), BF16),
            pltpu.VMEM((TILES + 1, 256, 256), BF16),
            pltpu.VMEM((TILES + 1, 2, 8, 128), F32),
            pltpu.VMEM((2, 256, TILES * 256), BF16),
            pltpu.VMEM((512, TILES * 256), BF16),
            pltpu.VMEM((1, 128), jnp.int32),
            pltpu.VMEM((128, 1, 128), jnp.int32),
            pltpu.VMEM((2, 2, 512, 128), F32),
            pltpu.VMEM((2, 512, 128), F32),
            pltpu.VMEM((2, 64, 8, 128), F32),
            pltpu.VMEM((2, 64, 8, 128), F32),
            pltpu.VMEM((2, 2, 8, 128), F32),
            dma((CHUNKS,)),
            dma, dma, dma((2,)), dma((2,)), dma((2,)), dma((2,)), dma, dma,
        ],
        compiler_params=pltpu.CompilerParams(
            collective_id=0, has_side_effects=True, vmem_limit_bytes=56 * 1024 * 1024
        ),
    )(x, momenta)


def clifford_table():
    zeros = np.zeros((4, 4))
    first = (zeros, np.array([[0, 0, 0, 1], [0, 0, 1, 0], [0, -1, 0, 0], [-1, 0, 0, 0]]))
    second = (np.array([[0, 0, 0, -1], [0, 0, 1, 0], [0, 1, 0, 0], [-1, 0, 0, 0]]), zeros)
    third = (zeros, np.array([[0, 0, 1, 0], [0, 0, 0, -1], [-1, 0, 0, 0], [0, 1, 0, 0]]))
    fourth = (np.array([[0, 0, 1, 0], [0, 0, 0, 1], [1, 0, 0, 0], [0, 1, 0, 0]]), zeros)
    basis = [first, second, third, fourth]
    tables_re = []
    tables_im = []
    for mask in range(16):
        matrix_re = np.identity(4)
        matrix_im = np.zeros((4, 4))
        for bit in range(4):
            if mask >> bit & 1:
                basis_re, basis_im = basis[bit]
                new_re = matrix_re @ basis_re - matrix_im @ basis_im
                new_im = matrix_re @ basis_im + matrix_im @ basis_re
                matrix_re, matrix_im = (new_re, new_im)
        tables_re.append(matrix_re)
        tables_im.append(matrix_im)
    return (np.stack(tables_re), np.stack(tables_im))


def select_gammas(gamma_index):
    table_re, table_im = clifford_table()
    onehot = (gamma_index[:, None] == jnp.arange(16, dtype=jnp.int32)[None, :]).astype(jnp.float32)
    high = lax.Precision.HIGHEST
    chosen_re = jnp.einsum(
        "gk,kst->gst", onehot, jnp.asarray(table_re, jnp.float32), precision=high
    )
    chosen_im = jnp.einsum(
        "gk,kst->gst", onehot, jnp.asarray(table_im, jnp.float32), precision=high
    )
    return (chosen_re, chosen_im)


def vertices_of(spec_re, spec_im, gamma_re, gamma_im):
    high = lax.Precision.HIGHEST
    count = spec_re.shape[0]
    split_re = spec_re.reshape(count, 4, 3, 12)
    split_im = spec_im.reshape(count, 4, 3, 12)
    turned_re = (
        jnp.einsum("gst,mtcb->mgscb", gamma_re, split_re, precision=high)
        - jnp.einsum("gst,mtcb->mgscb", gamma_im, split_im, precision=high)
    ).reshape(count, 16, 12, 12)
    turned_im = (
        jnp.einsum("gst,mtcb->mgscb", gamma_re, split_im, precision=high)
        + jnp.einsum("gst,mtcb->mgscb", gamma_im, split_re, precision=high)
    ).reshape(count, 16, 12, 12)
    result_re = jnp.einsum("mka,mgkb->mgab", spec_re, turned_re, precision=high) + jnp.einsum(
        "mka,mgkb->mgab", spec_im, turned_im, precision=high
    )
    result_im = jnp.einsum("mka,mgkb->mgab", spec_re, turned_im, precision=high) - jnp.einsum(
        "mka,mgkb->mgab", spec_im, turned_re, precision=high
    )
    return jnp.stack([result_re, result_im], axis=2)


def site_major(propagator):
    x = jnp.transpose(propagator, (1, 2, 0, 3)).reshape(144, 2, 64, 128)
    return jnp.transpose(x, (0, 2, 1, 3)).reshape(144, 128, 128)


def body(propagator, momenta, gamma_index):
    spectrum = spectrum_of(site_major(propagator), momenta)[:, :, :, :HALF]
    spectrum = jnp.transpose(spectrum, (2, 0, 1, 3)).reshape(4, 2, 12, 12)
    gamma_re, gamma_im = select_gammas(gamma_index)
    return vertices_of(spectrum[:, 0], spectrum[:, 1], gamma_re, gamma_im)


def solution(mesh):
    placed = (P(None, None, None, ("gx", "gz", "ta")), P(("gx", "gz", "ta"), None), P())
    return jax.shard_map(
        body,
        mesh=mesh,
        in_specs=placed,
        out_specs=P(("gx", "gz", "ta"), None, None, None, None),
        check_vma=False,
    )
```

time: 90.9 us -> 50.7 us (0.56)
  waiting for transfers between devices: 18.9 us -> 0 us
  starting transfers between devices: 10.9 us -> 0 us
  Pallas kernels: 48.7 us -> 42.5 us
  local copies, waits for them, and re-layouts: 7.13 us -> 3.42 us
    all_to_all x2 -> x0, waiting for transfers between devices: 18.9 us -> none  [summed_on_arrival(): lax.all_to_all(in_blocks(array, dim, devices), axis, 0, 0, tiled=True)]
    all_to_all x2 -> x0, starting transfers between devices: 10.9 us -> none  [summed_on_arrival(): lax.all_to_all(in_blocks(array, dim, devices), axis, 0, 0, tiled=True)]
    pallas_call x2 -> x1, Pallas kernels: 48.7 us -> 42.5 us  [spectrum_of(): pl.pallas_call(program_kernel, out_shape=jax.ShapeDtypeStruct((2, 2, 4, 1...]
    unnamed x13 -> x6, local copies, waits for them, and re-layouts: 2.45 us -> 0.01 us
    reshape x2, local copies, waits for them, and re-layouts: 1.47 us -> 0.11 us  [body(): spectrum = jnp.transpose(spectrum, (2, 0, 1, 3)).reshape(4, 2, 12, 12)]
  transfers between devices with their start and end apart: 2 -> 0, of which waited for: 2 -> 0; matrix products, arithmetic and copies ran while one was open for 0% -> 0% of each run, Pallas kernels for 0% -> 0%
where the time goes in v2:
time: 50.7 us; the launch traced here: 50.6 us
  Pallas kernels  42.5 us (84%)
  matrix products  4.48 us (9%)
  local copies, waits for them, and re-layouts  3.42 us (7%)
    pallas_call x1, Pallas kernels, spectrum_of(): pl.pallas_call(program_kernel, out_shape=jax.ShapeDtypeStruct((2, 2, 4, 1...  42.5 us
    another operation x1, local copies, waits for them, and re-layouts, vertices_of(): return jnp.stack([result_re, result_im], axis=2)  1.47 us

profile of v2, /device:TPU:1, one launch (start us, length us, event | category | flops | bytes accessed | tf_op | source)
XLA Modules:
  0.0 50.6 jit_solution(3263812596048658567)
XLA Ops:
  0.0 0.0 copy-start.1
  0.0 0.0 copy-start.2
  0.0 0.0 copy-start
  0.0 42.5 %shard_map.55 = f32[2,2,4,128]{3,2,1,0:T(4,128)} custom-call(f32[144,128,128]{2,1,0:T(8,128)} %bitcast.71, s32[4,4]{1,0:T(4,128)} %mom_smem.1), custom_call_target="tpu_custom_call" | custom-call | tf_op jit(solution)/shard_map/pallas_call | solution.py:300
  42.5 0.7 %slice_bitcast_fusion = f32[4,2,2,72]{3,0,2,1:T(4,128)S(1)} fusion(f32[2,2,4,128]{3,2,1,0:T(4,128)} %shard_map.55), kind=kLoop, calls=%fused_computation.24 | loop fusion | bytes 9216 | tf_op jit(solution)/shard_map/transpose | solution.py:395
  43.2 0.0 copy-done.1
  43.2 0.0 copy-done
  43.2 0.2 fusion.17
  43.4 0.0 copy-done.2
  43.4 0.2 fusion.16
  43.6 0.1 reshape.33
  43.7 0.6 %fusion.10 = f32[4,3,12,16,4]{3,2,4,1,0:T(8,128)S(1)} fusion(f32[16,4,4,1,1]{0,2,1,4,3:T(4,128)S(1)} %bitcast.80, f32[4,4,3,12,1]{3,0,2,1,4:T(4,128)S(1)} %bitcast.74), kind=kOutput, calls=%fused_computation.15 | convolution fusion | flops 442368 | bytes 40192 | tf_op jit(solution)/shard_map/gst,mtcb->mgscb/dot_general | solution.py:376
  44.3 0.6 %fusion.2 = f32[4,16,4,3,12]{1,4,2,3,0:T(8,128)S(1)} fusion(f32[4,3,12,16,4]{3,2,4,1,0:T(8,128)S(1)} %fusion.10, f32[16,4,4,1,1]{0,2,1,4,3:T(4,128)S(1)} %bitcast.78, f32[4,4,3,12,1]{3,0,2,1,4:T(4,128)S(1)} %bitcast.76), kind=kOutput, calls=%fused_computation.5 | convolution fusion | flops 451584 | bytes 77056 | tf_op jit(solution)/shard_map/gst,mtcb->mgscb/dot_general | solution.py:377
  44.9 0.2 copy.20
  45.1 0.4 copy.21
  45.4 0.6 %fusion.14 = f32[4,3,12,16,4]{3,2,4,1,0:T(8,128)S(1)} fusion(f32[16,4,4,1,1]{0,2,1,4,3:T(4,128)S(1)} %bitcast.81, f32[4,4,3,12,1]{3,0,2,1,4:T(4,128)S(1)} %bitcast.77), kind=kOutput, calls=%fused_computation.19 | convolution fusion | flops 442368 | bytes 40192 | tf_op jit(solution)/shard_map/gst,mtcb->mgscb/dot_general | solution.py:372
  46.0 0.6 %fusion.3 = f32[4,16,4,3,12]{1,4,2,3,0:T(8,128)S(1)} fusion(f32[4,3,12,16,4]{3,2,4,1,0:T(8,128)S(1)} %fusion.14, f32[16,4,4,1,1]{0,2,1,4,3:T(4,128)S(1)} %bitcast.79, f32[4,4,3,12,1]{3,0,2,1,4:T(4,128)S(1)} %bitcast.75), kind=kOutput, calls=%fused_computation.7 | convolution fusion | flops 451584 | bytes 77056 | tf_op jit(solution)/shard_map/gst,mtcb->mgscb/dot_general | solution.py:373
  46.6 0.2 copy.16
  46.8 0.4 copy.17
  47.1 0.5 fusion.8
  47.6 0.5 fusion.1
  48.1 0.5 fusion.6
  48.6 0.5 fusion
  49.0 0.1 pad_maximum_fusion
  49.1 1.5 %copy.24 = f32[4,16,2,12,12]{1,2,4,3,0:T(2,128)} copy(f32[4,16,2,12,12]{3,1,4,0,2:T(8,128)S(1)} %pad_maximum_fusion) | data formatting | bytes 147456 | tf_op jit(solution)/shard_map/stack | solution.py:385
  (4 shorter events, 0.0 us)
Async XLA Ops:
  0.0 43.2 %copy-start.1 = (f32[16,16]{0,1:T(8,128)S(1)}, f32[16,16]{0,1:T(8,128)}, u32[]{:S(2)}) copy-start(f32[16,16]{0,1:T(8,128)} %constant.7) | copy-start | bytes 3076
  0.0 43.4 %copy-start.2 = (f32[16,16]{0,1:T(8,128)S(1)}, f32[16,16]{0,1:T(8,128)}, u32[]{:S(2)}) copy-start(f32[16,16]{0,1:T(8,128)} %constant.8) | copy-start | bytes 3076
  0.0 43.2 %copy-start = (s32[16]{0:T(128)S(1)}, s32[16]{0:T(128)}, u32[]{:S(2)}) copy-start(s32[16]{0:T(128)} %param.7) | copy-start | bytes 196

commit v3 on v2

--- a/solution.py
+++ b/solution.py
@@ -70,16 +70,101 @@
     return split(jnp.where((row & 7) == (col >> 4), value, 0.0))
 
 
+def clifford_table():
+    zeros = np.zeros((4, 4))
+    first = (zeros, np.array([[0, 0, 0, 1], [0, 0, 1, 0], [0, -1, 0, 0], [-1, 0, 0, 0]]))
+    second = (np.array([[0, 0, 0, -1], [0, 0, 1, 0], [0, 1, 0, 0], [-1, 0, 0, 0]]), zeros)
+    third = (zeros, np.array([[0, 0, 1, 0], [0, 0, 0, -1], [-1, 0, 0, 0], [0, 1, 0, 0]]))
+    fourth = (np.array([[0, 0, 1, 0], [0, 0, 0, 1], [1, 0, 0, 0], [0, 1, 0, 0]]), zeros)
+    basis = [first, second, third, fourth]
+    tables_re = []
+    tables_im = []
+    for mask in range(16):
+        matrix_re = np.identity(4)
+        matrix_im = np.zeros((4, 4))
+        for bit in range(4):
+            if mask >> bit & 1:
+                basis_re, basis_im = basis[bit]
+                new_re = matrix_re @ basis_re - matrix_im @ basis_im
+                new_im = matrix_re @ basis_im + matrix_im @ basis_re
+                matrix_re, matrix_im = (new_re, new_im)
+        tables_re.append(matrix_re)
+        tables_im.append(matrix_im)
+    return (np.stack(tables_re), np.stack(tables_im))
+
+
+def structures():
+    table_re, table_im = clifford_table()
+    out = []
+    for re, im in zip(table_re, table_im, strict=True):
+        matrix = im if im.any() else re
+        columns = [int(np.flatnonzero(line)[0]) for line in matrix]
+        signs = [float(line[k]) for line, k in zip(matrix, columns, strict=True)]
+        out.append((bool(im.any()), columns, signs))
+    return out
+
+
+def write_vertices(spec, widen, slots, out_ref):
+    keep = iota((8, 128), 1) < HALF
+    lines = []
+    for sink in range(12):
+        half, k = divmod(sink, 6)
+        for part in range(2):
+            line = jnp.where(keep, spec[part, half], 0.0)
+            lines.append(pltpu.roll(line, 128 - 12 * k, 1) if k else line)
+    wide = jnp.concatenate(split(jnp.concatenate(lines, axis=0)), axis=1)
+    wide = jnp.dot(wide, widen[...], preferred_element_type=F32)
+    even = (iota((8, 384), 1) & 1) == 0
+    left_re = [wide[16 * k : 16 * k + 8, :384] for k in range(12)]
+    left_im = [wide[16 * k + 8 : 16 * k + 16, :384] for k in range(12)]
+    right, turned = [], []
+    for k in range(12):
+        re, im = wide[16 * k : 16 * k + 8, 384:], wide[16 * k + 8 : 16 * k + 16, 384:]
+        right.append(jnp.where(even, re, im))
+        turned.append(jnp.where(even, im, -re))
+
+    def pair(s, t):
+        total = None
+        for c in range(3):
+            a, b = 3 * s + c, 3 * t + c
+            term = left_re[a] * right[b] + left_im[a] * turned[b]
+            total = term if total is None else total + term
+        return total
+
+    pairs = {}
+    values = []
+    for imaginary, columns, signs in structures():
+        total = None
+        for s in range(4):
+            if (s, columns[s]) not in pairs:
+                pairs[s, columns[s]] = pair(s, columns[s])
+            term = pairs[s, columns[s]]
+            if total is None:
+                total = term if signs[s] > 0 else -term
+            else:
+                total = total + term if signs[s] > 0 else total - term
+        if imaginary:
+            total = jnp.where(even, -pltpu.roll(total, 383, 1), pltpu.roll(total, 1, 1))
+        values.append(total)
+    stacked = jnp.concatenate(split(jnp.concatenate(values, axis=0)), axis=0)
+    out = lax.dot_general(
+        stacked, slots[...], (((0,), (0,)), ((), ())), preferred_element_type=F32
+    )
+    for i in range(4):
+        out_ref[i] = out[:288, i * 128 : i * 128 + 16]
+
+
 def program_kernel(
-    x_hbm, mom_smem, out_ref,
-    sbuf, gh, gl, w_high, w_low, x_wave, yall, pick, row_buf, mom_all,
+    x_hbm, mom_smem, gamma_smem, out_ref,
+    sbuf, gh, gl, w_high, w_low, x_wave, yall, pick, mom_all,
+    before_buf, move_buf, widen, slots,
     zbuf, dbuf, hbuf, rbuf, spec,
     in_sems, mom_send, mom_recv, pair_send, pair_recv, far_send, far_recv, last_send, last_recv,
 ):
     gx, gz, ta = (lax.axis_index(name) for name in ("gx", "gz", "ta"))
     core, y_lo, z, y_hi = gz % 2, gz // 2, ta // 2, ta % 2
     y = y_hi * 2 + y_lo
-    me = (gx * 4 + gz) * 8 + ta
+    me = ((z * 4 + y) * 4 + gx) * 2 + core
     chip = (gx * 2 + y_lo) * 8 + ta
     xs = [gx] + [(gx + k) % 4 for k in range(1, 4)]
     ys = [y] + [(y + k) % 4 for k in range(1, 4)]
@@ -101,10 +186,15 @@
         dx, dy, dz = place
         return (xs[dx] * 2 + ys[dy] % 2) * 8 + tas[dy][dz]
 
-    others = [(place, dc) for place in chips for dc in (0, 1) if place != (0, 0, 0) or dc]
     barrier = pltpu.get_barrier_semaphore()
-    for place, dc in others:
-        pl.semaphore_signal(barrier, inc=1, device_id=device(place, dc), device_id_type=MESH)
+    stages = (
+        [((dx, 0, 0), dc) for dx in (2, 1, 3, 0) for dc in (0, 1) if dx or dc],
+        [((0, dy, 0), 0) for dy in (2, 1, 3)],
+        [((0, 0, dz), 0) for dz in (2, 1, 3)],
+    )
+    for stage in stages:
+        for place, dc in stage:
+            pl.semaphore_signal(barrier, inc=1, device_id=device(place, dc), device_id_type=MESH)
 
     def load(k):
         part = pl.ds(k * 8, 8)
@@ -116,7 +206,6 @@
     for i in range(4):
         for k in range(4):
             row = jnp.where(iota((1, 128), 1) == 4 * i + k, mom_smem[i, k], row)
-    row_buf[...] = row
     mom_all[me] = row
 
     fold_high, fold_low = fold_matrix()
@@ -143,27 +232,61 @@
                     gl[q, rows, lanes] = rest[2 * q + part]
         return carry
 
-    lax.fori_loop(0, CHUNKS // 2, fold_step, 0)
-
-    pl.semaphore_wait(barrier, 127)
-    for place, dc in others:
-        pltpu.make_async_remote_copy(
-            src_ref=row_buf, dst_ref=mom_all.at[me], send_sem=mom_send, recv_sem=mom_recv,
-            device_id=device(place, dc), device_id_type=MESH,
-        ).start()
-
-    lax.fori_loop(CHUNKS // 2, CHUNKS, fold_step, 0)
-
-    all_rows = mom_all.at[pl.ds(0, 127)]
-    pltpu.make_async_copy(all_rows, all_rows, mom_recv).wait()
+    def spread(k):
+        span = (1, 8, 32)[k]
+        rows = mom_all.at[pl.ds(me // span * span, span)]
+        for place, dc in stages[k]:
+            pltpu.make_async_remote_copy(
+                src_ref=rows, dst_ref=rows, send_sem=mom_send.at[k], recv_sem=mom_recv.at[k],
+                device_id=device(place, dc), device_id_type=MESH,
+            ).start()
+
+    def moved(k):
+        return mom_all.at[pl.ds(0, (7, 24, 96)[k])]
+
+    def arrived(k):
+        pltpu.make_async_copy(moved(k), moved(k), mom_recv.at[k]).wait()
+
+    lax.fori_loop(0, 3, fold_step, 0)
+    pl.semaphore_wait(barrier, 13)
+    spread(0)
+    lax.fori_loop(3, 11, fold_step, 0)
+    arrived(0)
+    spread(1)
+    lax.fori_loop(11, CHUNKS, fold_step, 0)
+    arrived(1)
+    spread(2)
+
+    before_buf[...] = (iota((512, 512), 0) < iota((512, 512), 1)).astype(F32).astype(BF16)
+    to_row = iota((512, 512), 0)
+    to_chip, to_core, own = to_row >> 3, (to_row >> 2) & 1, to_row & 3
+    to_y = (to_chip & 1) * 2 + ((to_chip >> 3) & 1)
+    source = own * 128 + ((to_chip >> 1) & 3) * 32 + to_y * 8 + (to_chip >> 4) * 2 + to_core
+    move_buf[...] = (source == iota((512, 512), 1)).astype(F32).astype(BF16)
+    lane = iota((128, 384), 1)
+    source_a = (lane * 2731) >> 16
+    source_b = (lane >> 1) - 12 * (((lane >> 1) * 5462) >> 16)
+    for k, wanted in enumerate((source_a, source_b)):
+        chosen = (iota((128, 384), 0) == wanted).astype(F32).astype(BF16)
+        widen[:128, k * 384 : k * 384 + 384] = chosen
+        widen[128:, k * 384 : k * 384 + 384] = chosen
+    gamma_row = jnp.full((1, 128), -1, jnp.int32)
+    for k in range(16):
+        gamma_row = jnp.where(iota((1, 128), 1) == k, gamma_smem[k], gamma_row)
+    row = iota((128, 128), 0)
+    for i in range(4):
+        chosen = ((row >> 3) == gamma_row) & ((row & 7) == core * 4 + i)
+        chosen = chosen.astype(F32).astype(BF16)
+        slots[:128, i * 128 : i * 128 + 128] = chosen
+        slots[128:, i * 128 : i * 128 + 128] = chosen
+    arrived(2)
 
     turned = jnp.transpose((mom_all[...].reshape(128, 128) & 31).astype(F32))
     mom = jnp.concatenate([turned[4 * i : 4 * i + 4] for i in range(4)], axis=1)
     ny = mom[1:2].astype(jnp.int32)
     cls = ((ny >> 1) & 3) + 4 * (ny & 1)
     member = (iota((8, 512), 0) == cls).astype(F32)
-    before = (iota((512, 512), 0) < iota((512, 512), 1)).astype(F32).astype(BF16)
-    ahead = jnp.dot(member.astype(BF16), before, preferred_element_type=F32)
+    ahead = jnp.dot(member.astype(BF16), before_buf[...], preferred_element_type=F32)
     slot = jnp.sum(member * ahead, axis=0, keepdims=True)
     ends = []
     start = jnp.int32(0)
@@ -175,19 +298,18 @@
     slot = slot.astype(jnp.int32)
     mom8 = jnp.concatenate([mom, jnp.zeros_like(mom)], axis=0).astype(BF16)
     digits = jnp.concatenate([slot >> 5, slot & 31] + [slot * 0] * 6, axis=0).astype(F32).astype(BF16)
-    to_row = iota((512, 512), 0)
-    to_chip, to_core, own = to_row >> 3, (to_row >> 2) & 1, to_row & 3
-    source = own * 128 + ((to_chip >> 3) * 2 + to_core) * 8 + (to_chip & 7)
-    move = (source == iota((512, 512), 1)).astype(F32).astype(BF16)
-    column = lax.dot_general(move, digits, NT, preferred_element_type=F32)
+    column = lax.dot_general(move_buf[...], digits, NT, preferred_element_type=F32)
     column = (column[:, 0:1] * 32.0 + column[:, 1:2]).astype(jnp.int32)
 
     def prepare(j):
         here = (iota((128, 512), 0) + j * 128 == slot).astype(F32).astype(BF16)
         sorted_mom = lax.dot_general(mom8, here, NT, preferred_element_type=F32).astype(jnp.int32)
         nx, ny, nz, nt = (sorted_mom[i : i + 1] for i in range(4))
-        site = iota((128, 128), 0)
-        pr, pi = wave(ny * (site >> 5) + nz * ((site >> 2) & 7) + nt * (site & 3))
+        site = iota((32, 128), 0)
+        zr, zi = wave(nz * (site >> 2) + nt * (site & 3))
+        yr, yi = wave(ny * iota((8, 128), 0))
+        pr = jnp.concatenate([zr * yr[k : k + 1] - zi * yi[k : k + 1] for k in range(4)], 0)
+        pi = jnp.concatenate([zr * yi[k : k + 1] + zi * yr[k : k + 1] for k in range(4)], 0)
         (prh, prl), (pih, pil) = split(pr), split(pi)
         w_high[j] = jnp.concatenate(
             [jnp.concatenate([prh, pih], 1), jnp.concatenate([-pih, prh], 1)], 0
@@ -284,23 +406,24 @@
         device_id=device((0, 0, 0), 1), device_id_type=MESH,
     )
     last.start()
-    pltpu.make_async_copy(all_rows, all_rows, mom_send).wait()
+    for k in range(3):
+        pltpu.make_async_copy(moved(k), moved(k), mom_send.at[k]).wait()
     for half in range(2):
         to_partner(half).wait_send()
         blocks = hbuf.at[half, pl.ds(0, 63)]
         pltpu.make_async_copy(blocks, blocks, far_send.at[half]).wait()
     last.wait()
-    value = spec[...]
-    out_ref[...] = jnp.where(core == 0, value[:, :, :4], value[:, :, 4:])
-
-
-def spectrum_of(x, momenta):
+    write_vertices(spec, widen, slots, out_ref)
+
+
+def vertices_kernel_call(x, momenta, gamma_index):
     vmem = pl.BlockSpec(memory_space=pltpu.VMEM)
     dma = pltpu.SemaphoreType.DMA
     return pl.pallas_call(
         program_kernel,
-        out_shape=jax.ShapeDtypeStruct((2, 2, 4, 128), F32),
-        in_specs=[pl.BlockSpec(memory_space=pl.ANY), pl.BlockSpec(memory_space=pltpu.SMEM)],
+        out_shape=jax.ShapeDtypeStruct((4, 288, 16), F32),
+        in_specs=[pl.BlockSpec(memory_space=pl.ANY)]
+        + [pl.BlockSpec(memory_space=pltpu.SMEM)] * 2,
         out_specs=vmem,
         scratch_shapes=[
             pltpu.VMEM((144, 128, 128), F32),
@@ -311,78 +434,23 @@
             pltpu.VMEM((TILES + 1, 2, 8, 128), F32),
             pltpu.VMEM((2, 256, TILES * 256), BF16),
             pltpu.VMEM((512, TILES * 256), BF16),
-            pltpu.VMEM((1, 128), jnp.int32),
             pltpu.VMEM((128, 1, 128), jnp.int32),
+            pltpu.VMEM((512, 512), BF16),
+            pltpu.VMEM((512, 512), BF16),
+            pltpu.VMEM((256, 768), BF16),
+            pltpu.VMEM((256, 512), BF16),
             pltpu.VMEM((2, 2, 512, 128), F32),
             pltpu.VMEM((2, 512, 128), F32),
             pltpu.VMEM((2, 64, 8, 128), F32),
             pltpu.VMEM((2, 64, 8, 128), F32),
             pltpu.VMEM((2, 2, 8, 128), F32),
             dma((CHUNKS,)),
-            dma, dma, dma((2,)), dma((2,)), dma((2,)), dma((2,)), dma, dma,
+            dma((3,)), dma((3,)), dma((2,)), dma((2,)), dma((2,)), dma((2,)), dma, dma,
         ],
         compiler_params=pltpu.CompilerParams(
             collective_id=0, has_side_effects=True, vmem_limit_bytes=56 * 1024 * 1024
         ),
-    )(x, momenta)
-
-
-def clifford_table():
-    zeros = np.zeros((4, 4))
-    first = (zeros, np.array([[0, 0, 0, 1], [0, 0, 1, 0], [0, -1, 0, 0], [-1, 0, 0, 0]]))
-    second = (np.array([[0, 0, 0, -1], [0, 0, 1, 0], [0, 1, 0, 0], [-1, 0, 0, 0]]), zeros)
-    third = (zeros, np.array([[0, 0, 1, 0], [0, 0, 0, -1], [-1, 0, 0, 0], [0, 1, 0, 0]]))
-    fourth = (np.array([[0, 0, 1, 0], [0, 0, 0, 1], [1, 0, 0, 0], [0, 1, 0, 0]]), zeros)
-    basis = [first, second, third, fourth]
-    tables_re = []
-    tables_im = []
-    for mask in range(16):
-        matrix_re = np.identity(4)
-        matrix_im = np.zeros((4, 4))
-        for bit in range(4):
-            if mask >> bit & 1:
-                basis_re, basis_im = basis[bit]
-                new_re = matrix_re @ basis_re - matrix_im @ basis_im
-                new_im = matrix_re @ basis_im + matrix_im @ basis_re
-                matrix_re, matrix_im = (new_re, new_im)
-        tables_re.append(matrix_re)
-        tables_im.append(matrix_im)
-    return (np.stack(tables_re), np.stack(tables_im))
-
-
-def select_gammas(gamma_index):
-    table_re, table_im = clifford_table()
-    onehot = (gamma_index[:, None] == jnp.arange(16, dtype=jnp.int32)[None, :]).astype(jnp.float32)
-    high = lax.Precision.HIGHEST
-    chosen_re = jnp.einsum(
-        "gk,kst->gst", onehot, jnp.asarray(table_re, jnp.float32), precision=high
-    )
-    chosen_im = jnp.einsum(
-        "gk,kst->gst", onehot, jnp.asarray(table_im, jnp.float32), precision=high
-    )
-    return (chosen_re, chosen_im)
-
-
-def vertices_of(spec_re, spec_im, gamma_re, gamma_im):
-    high = lax.Precision.HIGHEST
-    count = spec_re.shape[0]
-    split_re = spec_re.reshape(count, 4, 3, 12)
-    split_im = spec_im.reshape(count, 4, 3, 12)
-    turned_re = (
-        jnp.einsum("gst,mtcb->mgscb", gamma_re, split_re, precision=high)
-        - jnp.einsum("gst,mtcb->mgscb", gamma_im, split_im, precision=high)
-    ).reshape(count, 16, 12, 12)
-    turned_im = (
-        jnp.einsum("gst,mtcb->mgscb", gamma_re, split_im, precision=high)
-        + jnp.einsum("gst,mtcb->mgscb", gamma_im, split_re, precision=high)
-    ).reshape(count, 16, 12, 12)
-    result_re = jnp.einsum("mka,mgkb->mgab", spec_re, turned_re, precision=high) + jnp.einsum(
-        "mka,mgkb->mgab", spec_im, turned_im, precision=high
-    )
-    result_im = jnp.einsum("mka,mgkb->mgab", spec_re, turned_im, precision=high) - jnp.einsum(
-        "mka,mgkb->mgab", spec_im, turned_re, precision=high
-    )
-    return jnp.stack([result_re, result_im], axis=2)
+    )(x, momenta, gamma_index)
 
 
 def site_major(propagator):
@@ -391,10 +459,8 @@
 
 
 def body(propagator, momenta, gamma_index):
-    spectrum = spectrum_of(site_major(propagator), momenta)[:, :, :, :HALF]
-    spectrum = jnp.transpose(spectrum, (2, 0, 1, 3)).reshape(4, 2, 12, 12)
-    gamma_re, gamma_im = select_gammas(gamma_index)
-    return vertices_of(spectrum[:, 0], spectrum[:, 1], gamma_re, gamma_im)
+    out = vertices_kernel_call(site_major(propagator), momenta, gamma_index)
+    return jnp.transpose(out.reshape(4, 12, 12, 2, 16), (0, 4, 3, 1, 2))
 
 
 def solution(mesh):

time: 50.7 us -> 45 us (0.89)
  matrix products: 4.48 us -> 0 us
  local copies, waits for them, and re-layouts: 3.42 us -> 1.92 us
    dot_general x8 -> x0, matrix products: 4.1 us -> none  [the longest x1 0.57 us: vertices_of(): jnp.einsum('gst,mtcb->mgscb', gamma_im, split_re, precision=high)]
    unnamed x6 -> x1, local copies, waits for them, and re-layouts: 0.01 us -> 1.92 us
    another operation x1 -> x0, local copies, waits for them, and re-layouts: 1.47 us -> none  [vertices_of(): return jnp.stack([result_re, result_im], axis=2)]
    reshape x4 -> x0, local copies, waits for them, and re-layouts: 0.83 us -> none  [the longest x1 0.36 us: vertices_of(): turned_re = (jnp.einsum('gst,mtcb->mgscb', gamma_re, split_re, precision=...]
    transpose x1 -> x0, local copies, waits for them, and re-layouts: 0.7 us -> none  [body(): spectrum = jnp.transpose(spectrum, (2, 0, 1, 3)).reshape(4, 2, 12, 12)]
where the time goes in v3:
time: 45 us; the launch traced here: 44.9 us
  Pallas kernels  42.9 us (95%)
  local copies, waits for them, and re-layouts  1.92 us (4%)
    pallas_call x1, Pallas kernels, vertices_kernel_call(): pl.pallas_call(program_kernel, out_shape=jax.ShapeDtypeStruct((4, 288, 16...  42.9 us
    unnamed x1, local copies, waits for them, and re-layouts  1.92 us

profile of v3, /device:TPU:1, one launch (start us, length us, event | category | flops | bytes accessed | tf_op | source)
XLA Modules:
  0.0 44.9 jit_solution(16972186757493983621)
XLA Ops:
  0.0 42.9 %shard_map.37 = f32[4,288,16]{2,1,0:T(8,128)} custom-call(f32[144,128,128]{2,1,0:T(8,128)} %bitcast.10, s32[4,4]{1,0:T(4,128)} %mom_smem.1, s32[16]{0:T(128)} %gamma_smem.1), custom_call_target="tpu_custom_call" | custom-call | tf_op jit(solution)/shard_map/pallas_call | solution.py:422
  42.9 1.9 %copy.6 = f32[4,16,2,12,12]{1,2,4,3,0:T(2,128)} copy(f32[4,16,2,12,12]{1,2,4,3,0:T(2,128)} %bitcast.11) | data formatting | bytes 147456

commit v4 on v3

--- a/solution.py
+++ b/solution.py
@@ -156,7 +156,7 @@
 
 def program_kernel(
     x_hbm, mom_smem, gamma_smem, out_ref,
-    sbuf, gh, gl, w_high, w_low, x_wave, yall, pick, mom_all,
+    sbuf, gh, gl, w_high, w_low, x_wave, raw_even, raw_odd, yall, pick, mom_all,
     before_buf, move_buf, widen, slots,
     zbuf, dbuf, hbuf, rbuf, spec,
     in_sems, mom_send, mom_recv, pair_send, pair_recv, far_send, far_recv, last_send, last_recv,
@@ -187,14 +187,9 @@
         return (xs[dx] * 2 + ys[dy] % 2) * 8 + tas[dy][dz]
 
     barrier = pltpu.get_barrier_semaphore()
-    stages = (
-        [((dx, 0, 0), dc) for dx in (2, 1, 3, 0) for dc in (0, 1) if dx or dc],
-        [((0, dy, 0), 0) for dy in (2, 1, 3)],
-        [((0, 0, dz), 0) for dz in (2, 1, 3)],
-    )
-    for stage in stages:
-        for place, dc in stage:
-            pl.semaphore_signal(barrier, inc=1, device_id=device(place, dc), device_id_type=MESH)
+    others = [(place, dc) for place in chips for dc in (0, 1) if place != (0, 0, 0) or dc]
+    for place, dc in others:
+        pl.semaphore_signal(barrier, inc=1, device_id=device(place, dc), device_id_type=MESH)
 
     def load(k):
         part = pl.ds(k * 8, 8)
@@ -232,37 +227,21 @@
                     gl[q, rows, lanes] = rest[2 * q + part]
         return carry
 
-    def spread(k):
-        span = (1, 8, 32)[k]
-        rows = mom_all.at[pl.ds(me // span * span, span)]
-        for place, dc in stages[k]:
-            pltpu.make_async_remote_copy(
-                src_ref=rows, dst_ref=rows, send_sem=mom_send.at[k], recv_sem=mom_recv.at[k],
-                device_id=device(place, dc), device_id_type=MESH,
-            ).start()
-
-    def moved(k):
-        return mom_all.at[pl.ds(0, (7, 24, 96)[k])]
-
-    def arrived(k):
-        pltpu.make_async_copy(moved(k), moved(k), mom_recv.at[k]).wait()
-
-    lax.fori_loop(0, 3, fold_step, 0)
-    pl.semaphore_wait(barrier, 13)
-    spread(0)
-    lax.fori_loop(3, 11, fold_step, 0)
-    arrived(0)
-    spread(1)
-    lax.fori_loop(11, CHUNKS, fold_step, 0)
-    arrived(1)
-    spread(2)
+    lax.fori_loop(0, 10, fold_step, 0)
+    pl.semaphore_wait(barrier, 127)
+    for place, dc in others:
+        pltpu.make_async_remote_copy(
+            src_ref=mom_all.at[me], dst_ref=mom_all.at[me], send_sem=mom_send, recv_sem=mom_recv,
+            device_id=device(place, dc), device_id_type=MESH,
+        ).start()
+    lax.fori_loop(10, CHUNKS, fold_step, 0)
 
     before_buf[...] = (iota((512, 512), 0) < iota((512, 512), 1)).astype(F32).astype(BF16)
-    to_row = iota((512, 512), 0)
+    to_row = iota((512, 512), 1)
     to_chip, to_core, own = to_row >> 3, (to_row >> 2) & 1, to_row & 3
     to_y = (to_chip & 1) * 2 + ((to_chip >> 3) & 1)
     source = own * 128 + ((to_chip >> 1) & 3) * 32 + to_y * 8 + (to_chip >> 4) * 2 + to_core
-    move_buf[...] = (source == iota((512, 512), 1)).astype(F32).astype(BF16)
+    move_buf[...] = (source == iota((512, 512), 0)).astype(F32).astype(BF16)
     lane = iota((128, 384), 1)
     source_a = (lane * 2731) >> 16
     source_b = (lane >> 1) - 12 * (((lane >> 1) * 5462) >> 16)
@@ -279,11 +258,15 @@
         chosen = chosen.astype(F32).astype(BF16)
         slots[:128, i * 128 : i * 128 + 128] = chosen
         slots[128:, i * 128 : i * 128 + 128] = chosen
-    arrived(2)
+    all_rows = mom_all.at[pl.ds(0, 127)]
+    pltpu.make_async_copy(all_rows, all_rows, mom_recv).wait()
 
     turned = jnp.transpose((mom_all[...].reshape(128, 128) & 31).astype(F32))
     mom = jnp.concatenate([turned[4 * i : 4 * i + 4] for i in range(4)], axis=1)
-    ny = mom[1:2].astype(jnp.int32)
+    mom8 = jnp.concatenate([mom, jnp.zeros_like(mom)], axis=0).astype(BF16)
+    mom8 = jnp.dot(mom8, move_buf[...], preferred_element_type=F32)
+    ny = mom8[1:2].astype(jnp.int32)
+    mom8 = mom8.astype(BF16)
     cls = ((ny >> 1) & 3) + 4 * (ny & 1)
     member = (iota((8, 512), 0) == cls).astype(F32)
     ahead = jnp.dot(member.astype(BF16), before_buf[...], preferred_element_type=F32)
@@ -296,13 +279,9 @@
         start = start + ((count + 127) >> 7)
         ends.append(start)
     slot = slot.astype(jnp.int32)
-    mom8 = jnp.concatenate([mom, jnp.zeros_like(mom)], axis=0).astype(BF16)
-    digits = jnp.concatenate([slot >> 5, slot & 31] + [slot * 0] * 6, axis=0).astype(F32).astype(BF16)
-    column = lax.dot_general(move_buf[...], digits, NT, preferred_element_type=F32)
-    column = (column[:, 0:1] * 32.0 + column[:, 1:2]).astype(jnp.int32)
-
     def prepare(j):
         here = (iota((128, 512), 0) + j * 128 == slot).astype(F32).astype(BF16)
+        pick[pl.ds(pl.multiple_of(j * 128, 128), 128)] = here
         sorted_mom = lax.dot_general(mom8, here, NT, preferred_element_type=F32).astype(jnp.int32)
         nx, ny, nz, nt = (sorted_mom[i : i + 1] for i in range(4))
         site = iota((32, 128), 0)
@@ -328,38 +307,37 @@
         rows = pl.ds(half * HALF * 8, HALF * 8)
         high = gh[q, rows]
         top = w_high[j]
-        out = (
+        return (
             jnp.dot(high, top, preferred_element_type=F32)
             + jnp.dot(gl[q, rows], top, preferred_element_type=F32)
             + jnp.dot(high, w_low[j], preferred_element_type=F32)
         )
+
+    def finish(raw, j, half):
         xr, xi = x_wave[j, 0], x_wave[j, 1]
-        re = out[:, :128].reshape(HALF, 8, 128)
-        im = out[:, 128:].reshape(HALF, 8, 128)
-        lanes = pl.ds(pl.multiple_of(j * 256, 256), 128)
-        lanes_low = pl.ds(pl.multiple_of(j * 256 + 128, 128), 128)
+        re = raw[:, :128].reshape(HALF, 8, 128)
+        im = raw[:, 128:].reshape(HALF, 8, 128)
+        lanes = pl.ds(pl.multiple_of(j * 128, 128), 128)
         for part, value in enumerate((re * xr - im * xi, re * xi + im * xr)):
             first, rest = split(sum_over_x(value))
-            to = pl.ds(part * 128, HALF)
-            yall[half, to, lanes] = first
-            yall[half, to, lanes_low] = rest
-
-    def choose(j):
-        lanes = pl.ds(pl.multiple_of(j * 256, 256), 128)
-        lanes_low = pl.ds(pl.multiple_of(j * 256 + 128, 128), 128)
-        chosen = (iota((512, 128), 1) + j * 128 == column).astype(F32).astype(BF16)
-        pick[:, lanes] = chosen
-        pick[:, lanes_low] = chosen
-
-    def first_step(j, carry):
-        multiply(j, 0)
-        prepare(j + 1)
-        choose(j)
-        return carry
-
-    def second_step(j, carry):
-        multiply(j, 1)
-        return carry
+            yall[half, pl.ds(part * HALF, HALF), lanes] = first
+            yall[half, pl.ds((2 + part) * HALF, HALF), lanes] = rest
+
+    def two_tiles(half):
+        def step(i, carry):
+            out = multiply(2 * i, half)
+            finish(raw_odd, (2 * i + TILES) % (TILES + 1), half)
+            if half == 0:
+                prepare(2 * i + 2)
+            raw_even[...] = out
+            out = multiply(2 * i + 1, half)
+            finish(raw_even, 2 * i, half)
+            if half == 0:
+                prepare(2 * i + 3)
+            raw_odd[...] = out
+            return carry
+
+        return step
 
     def to_partner(half):
         return pltpu.make_async_remote_copy(
@@ -369,9 +347,14 @@
         )
 
     def restore(half):
-        back = lax.dot_general(pick[...], yall[half], NT, preferred_element_type=F32)
-        zbuf[half, 0] = back[:, :128]
-        zbuf[half, 1] = back[:, 128:]
+        back = jnp.dot(
+            yall[half, :, : TILES * 128], pick[: TILES * 128], preferred_element_type=F32
+        )
+        back = back[: 2 * HALF] + back[2 * HALF :]
+        fill = jnp.zeros((128 - HALF, 512), F32)
+        for part in range(2):
+            rows = jnp.concatenate([back[part * HALF : (part + 1) * HALF], fill], axis=0)
+            zbuf[half, part] = jnp.transpose(rows)
         to_partner(half).start()
 
     def send_far(half):
@@ -392,11 +375,13 @@
         spec[core, half] = jnp.sum(rbuf[half], axis=0)
 
     prepare(jnp.int32(0))
-    lax.fori_loop(0, TILES, first_step, 0)
+    prepare(jnp.int32(1))
+    steps = (TILES + 1) // 2
+    lax.fori_loop(0, steps, two_tiles(0), 0)
     restore(0)
-    lax.fori_loop(0, TILES // 2, second_step, 0)
+    lax.fori_loop(0, steps // 2, two_tiles(1), 0)
     send_far(0)
-    lax.fori_loop(TILES // 2, TILES, second_step, 0)
+    lax.fori_loop(steps // 2, steps, two_tiles(1), 0)
     restore(1)
     send_far(1)
     wait_far(0)
@@ -406,8 +391,7 @@
         device_id=device((0, 0, 0), 1), device_id_type=MESH,
     )
     last.start()
-    for k in range(3):
-        pltpu.make_async_copy(moved(k), moved(k), mom_send.at[k]).wait()
+    pltpu.make_async_copy(all_rows, all_rows, mom_send).wait()
     for half in range(2):
         to_partner(half).wait_send()
         blocks = hbuf.at[half, pl.ds(0, 63)]
@@ -429,11 +413,13 @@
             pltpu.VMEM((144, 128, 128), F32),
             pltpu.VMEM((8, 1152, 256), BF16),
             pltpu.VMEM((8, 1152, 256), BF16),
-            pltpu.VMEM((TILES + 1, 256, 256), BF16),
-            pltpu.VMEM((TILES + 1, 256, 256), BF16),
-            pltpu.VMEM((TILES + 1, 2, 8, 128), F32),
-            pltpu.VMEM((2, 256, TILES * 256), BF16),
-            pltpu.VMEM((512, TILES * 256), BF16),
+            pltpu.VMEM((TILES + 3, 256, 256), BF16),
+            pltpu.VMEM((TILES + 3, 256, 256), BF16),
+            pltpu.VMEM((TILES + 3, 2, 8, 128), F32),
+            pltpu.VMEM((HALF * 8, 256), F32),
+            pltpu.VMEM((HALF * 8, 256), F32),
+            pltpu.VMEM((2, 4 * HALF, (TILES + 1) * 128), BF16),
+            pltpu.VMEM(((TILES + 3) * 128, 512), BF16),
             pltpu.VMEM((128, 1, 128), jnp.int32),
             pltpu.VMEM((512, 512), BF16),
             pltpu.VMEM((512, 512), BF16),
@@ -445,7 +431,7 @@
             pltpu.VMEM((2, 64, 8, 128), F32),
             pltpu.VMEM((2, 2, 8, 128), F32),
             dma((CHUNKS,)),
-            dma((3,)), dma((3,)), dma((2,)), dma((2,)), dma((2,)), dma((2,)), dma, dma,
+            dma, dma, dma((2,)), dma((2,)), dma((2,)), dma((2,)), dma, dma,
         ],
         compiler_params=pltpu.CompilerParams(
             collective_id=0, has_side_effects=True, vmem_limit_bytes=56 * 1024 * 1024

time: 45 us -> 42.8 us (0.951)
  Pallas kernels: 42.9 us -> 40.7 us
    pallas_call x1, Pallas kernels: 42.9 us -> 40.7 us  [vertices_kernel_call(): pl.pallas_call(program_kernel, out_shape=jax.ShapeDtypeStruct((4, 288, 16...]
where the time goes in v4:
time: 42.8 us; the launch traced here: 42.6 us
  Pallas kernels  40.7 us (95%)
  local copies, waits for them, and re-layouts  1.92 us (4%)
    pallas_call x1, Pallas kernels, vertices_kernel_call(): pl.pallas_call(program_kernel, out_shape=jax.ShapeDtypeStruct((4, 288, 16...  40.7 us
    unnamed x1, local copies, waits for them, and re-layouts  1.92 us

profile of v4, /device:TPU:1, one launch (start us, length us, event | category | flops | bytes accessed | tf_op | source)
XLA Modules:
  0.0 42.6 jit_solution(3004386466682187734)
XLA Ops:
  0.0 40.7 %shard_map.37 = f32[4,288,16]{2,1,0:T(8,128)} custom-call(f32[144,128,128]{2,1,0:T(8,128)} %bitcast.10, s32[4,4]{1,0:T(4,128)} %mom_smem.1, s32[16]{0:T(128)} %gamma_smem.1), custom_call_target="tpu_custom_call" | custom-call | tf_op jit(solution)/shard_map/pallas_call | solution.py:406
  40.7 1.9 %copy.6 = f32[4,16,2,12,12]{1,2,4,3,0:T(2,128)} copy(f32[4,16,2,12,12]{1,2,4,3,0:T(2,128)} %bitcast.11) | data formatting | bytes 147456

commit v5 on v4

--- a/solution.py
+++ b/solution.py
@@ -156,7 +156,7 @@
 
 def program_kernel(
     x_hbm, mom_smem, gamma_smem, out_ref,
-    sbuf, gh, gl, w_high, w_low, x_wave, raw_even, raw_odd, yall, pick, mom_all,
+    sbuf, gh, gl, w_high, w_low, x_wave, raw_a, raw_b, raw_c, raw_d, yall, pick, mom_all,
     before_buf, move_buf, widen, slots,
     zbuf, dbuf, hbuf, rbuf, spec,
     in_sems, mom_send, mom_recv, pair_send, pair_recv, far_send, far_recv, last_send, last_recv,
@@ -186,6 +186,7 @@
         dx, dy, dz = place
         return (xs[dx] * 2 + ys[dy] % 2) * 8 + tas[dy][dz]
 
+    raws = (raw_a, raw_b, raw_c, raw_d)
     barrier = pltpu.get_barrier_semaphore()
     others = [(place, dc) for place in chips for dc in (0, 1) if place != (0, 0, 0) or dc]
     for place, dc in others:
@@ -323,18 +324,24 @@
             yall[half, pl.ds(part * HALF, HALF), lanes] = first
             yall[half, pl.ds((2 + part) * HALF, HALF), lanes] = rest
 
-    def two_tiles(half):
+    def four_tiles(half):
         def step(i, carry):
-            out = multiply(2 * i, half)
-            finish(raw_odd, (2 * i + TILES) % (TILES + 1), half)
+            first = [multiply(4 * i + k, half) for k in (0, 1)]
+            for k in (2, 3):
+                finish(raws[k], (4 * i + k + 2 * TILES - 2) % (TILES + 1), half)
             if half == 0:
-                prepare(2 * i + 2)
-            raw_even[...] = out
-            out = multiply(2 * i + 1, half)
-            finish(raw_even, 2 * i, half)
+                prepare(4 * i + 4)
+                prepare(4 * i + 5)
+            for k in (0, 1):
+                raws[k][...] = first[k]
+            second = [multiply(4 * i + k, half) for k in (2, 3)]
+            for k in (0, 1):
+                finish(raws[k], 4 * i + k, half)
             if half == 0:
-                prepare(2 * i + 3)
-            raw_odd[...] = out
+                prepare(4 * i + 6)
+                prepare(4 * i + 7)
+            for k in (2, 3):
+                raws[k][...] = second[k - 2]
             return carry
 
         return step
@@ -347,6 +354,7 @@
         )
 
     def restore(half):
+        finish(raws[2], TILES - 1, half)
         back = jnp.dot(
             yall[half, :, : TILES * 128], pick[: TILES * 128], preferred_element_type=F32
         )
@@ -374,14 +382,13 @@
         pltpu.make_async_copy(blocks, blocks, far_recv.at[half]).wait()
         spec[core, half] = jnp.sum(rbuf[half], axis=0)
 
-    prepare(jnp.int32(0))
-    prepare(jnp.int32(1))
-    steps = (TILES + 1) // 2
-    lax.fori_loop(0, steps, two_tiles(0), 0)
+    for k in range(4):
+        prepare(jnp.int32(k))
+    lax.fori_loop(0, 3, four_tiles(0), 0)
     restore(0)
-    lax.fori_loop(0, steps // 2, two_tiles(1), 0)
+    lax.fori_loop(0, 2, four_tiles(1), 0)
     send_far(0)
-    lax.fori_loop(steps // 2, steps, two_tiles(1), 0)
+    lax.fori_loop(2, 3, four_tiles(1), 0)
     restore(1)
     send_far(1)
     wait_far(0)
@@ -405,7 +412,7 @@
     dma = pltpu.SemaphoreType.DMA
     return pl.pallas_call(
         program_kernel,
-        out_shape=jax.ShapeDtypeStruct((4, 288, 16), F32),
+        out_shape=pltpu.VMEM((4, 288, 16), F32),
         in_specs=[pl.BlockSpec(memory_space=pl.ANY)]
         + [pl.BlockSpec(memory_space=pltpu.SMEM)] * 2,
         out_specs=vmem,
@@ -413,13 +420,12 @@
             pltpu.VMEM((144, 128, 128), F32),
             pltpu.VMEM((8, 1152, 256), BF16),
             pltpu.VMEM((8, 1152, 256), BF16),
-            pltpu.VMEM((TILES + 3, 256, 256), BF16),
-            pltpu.VMEM((TILES + 3, 256, 256), BF16),
-            pltpu.VMEM((TILES + 3, 2, 8, 128), F32),
-            pltpu.VMEM((HALF * 8, 256), F32),
-            pltpu.VMEM((HALF * 8, 256), F32),
+            pltpu.VMEM((TILES + 5, 256, 256), BF16),
+            pltpu.VMEM((TILES + 5, 256, 256), BF16),
+            pltpu.VMEM((TILES + 5, 2, 8, 128), F32),
+            *[pltpu.VMEM((HALF * 8, 256), F32)] * 4,
             pltpu.VMEM((2, 4 * HALF, (TILES + 1) * 128), BF16),
-            pltpu.VMEM(((TILES + 3) * 128, 512), BF16),
+            pltpu.VMEM(((TILES + 5) * 128, 512), BF16),
             pltpu.VMEM((128, 1, 128), jnp.int32),
             pltpu.VMEM((512, 512), BF16),
             pltpu.VMEM((512, 512), BF16),

time: 42.8 us -> 40.1 us (0.937)
  Pallas kernels: 40.7 us -> 39.2 us
  local copies, waits for them, and re-layouts: 1.92 us -> 0.82 us
    pallas_call x1, Pallas kernels: 40.7 us -> 39.2 us  [vertices_kernel_call(): pl.pallas_call(program_kernel, out_shape=pltpu.VMEM((4, 288, 16), F32), i...]
    unnamed x1, local copies, waits for them, and re-layouts: 1.92 us -> 0.82 us
where the time goes in v5:
time: 40.1 us; the launch traced here: 40 us
  Pallas kernels  39.2 us (98%)
  local copies, waits for them, and re-layouts  0.82 us (2%)
    pallas_call x1, Pallas kernels, vertices_kernel_call(): pl.pallas_call(program_kernel, out_shape=pltpu.VMEM((4, 288, 16), F32), i...  39.2 us
    unnamed x1, local copies, waits for them, and re-layouts  0.82 us

profile of v5, /device:TPU:1, one launch (start us, length us, event | category | flops | bytes accessed | tf_op | source)
XLA Modules:
  0.0 40.0 jit_solution(2561904024390733563)
XLA Ops:
  0.0 39.2 %shard_map.37 = f32[4,288,16]{2,1,0:T(8,128)S(1)} custom-call(f32[144,128,128]{2,1,0:T(8,128)} %bitcast.11, s32[4,4]{1,0:T(4,128)} %mom_smem.1, s32[16]{0:T(128)} %gamma_smem.1), custom_call_target="tpu_custom_call" | custom-call | tf_op jit(solution)/shard_map/pallas_call | solution.py:413
  39.2 0.8 %copy.6 = f32[4,16,2,12,12]{1,2,4,3,0:T(2,128)} copy(f32[4,16,2,12,12]{1,2,4,3,0:T(2,128)S(1)} %bitcast.10) | data formatting | bytes 147456

commit v6 on v5

--- a/solution.py
+++ b/solution.py
@@ -285,11 +285,17 @@
         pick[pl.ds(pl.multiple_of(j * 128, 128), 128)] = here
         sorted_mom = lax.dot_general(mom8, here, NT, preferred_element_type=F32).astype(jnp.int32)
         nx, ny, nz, nt = (sorted_mom[i : i + 1] for i in range(4))
-        site = iota((32, 128), 0)
-        zr, zi = wave(nz * (site >> 2) + nt * (site & 3))
-        yr, yi = wave(ny * iota((8, 128), 0))
-        pr = jnp.concatenate([zr * yr[k : k + 1] - zi * yi[k : k + 1] for k in range(4)], 0)
-        pi = jnp.concatenate([zr * yi[k : k + 1] + zi * yr[k : k + 1] for k in range(4)], 0)
+        k, r = iota((16, 128), 0), iota((8, 128), 0)
+        phases = (
+            nz * (r >> 2) + nt * (r & 3),
+            ny * (k >> 2) + nz * (2 * (k & 3)),
+            nx * (gx * 8 + r) + nz * (gz * 8) + nt * (ta * 4),
+        )
+        re, im = wave(jnp.concatenate(phases, axis=0))
+        lr, li = re[:8], im[:8]
+        rows = [(re[n : n + 1], im[n : n + 1]) for n in range(8, 24)]
+        pr = jnp.concatenate([lr * hr - li * hi for hr, hi in rows], 0)
+        pi = jnp.concatenate([lr * hi + li * hr for hr, hi in rows], 0)
         (prh, prl), (pih, pil) = split(pr), split(pi)
         w_high[j] = jnp.concatenate(
             [jnp.concatenate([prh, pih], 1), jnp.concatenate([-pih, prh], 1)], 0
@@ -297,9 +303,8 @@
         w_low[j] = jnp.concatenate(
             [jnp.concatenate([prl, pil], 1), jnp.concatenate([-pil, prl], 1)], 0
         )
-        xr, xi = wave(nx * (gx * 8 + iota((8, 128), 0)) + nz * (gz * 8) + nt * (ta * 4))
-        x_wave[j, 0] = xr
-        x_wave[j, 1] = xi
+        x_wave[j, 0] = re[24:]
+        x_wave[j, 1] = im[24:]
 
     def multiply(j, half):
         q = jnp.int32(0)
@@ -324,27 +329,30 @@
             yall[half, pl.ds(part * HALF, HALF), lanes] = first
             yall[half, pl.ds((2 + part) * HALF, HALF), lanes] = rest
 
-    def four_tiles(half):
+    def four_tiles(i, half, ahead):
+        out = [multiply(4 * i + k, half) for k in (0, 1)]
+        for k in (2, 3):
+            finish(raws[k], (4 * i + k + 2 * TILES - 2) % (TILES + 1), half)
+        if ahead:
+            prepare(4 * i + 4)
+            prepare(4 * i + 5)
+        for k in (0, 1):
+            raws[k][...] = out[k]
+        out = [multiply(4 * i + k, half) for k in (2, 3)]
+        for k in (0, 1):
+            finish(raws[k], 4 * i + k, half)
+        if ahead:
+            prepare(4 * i + 6)
+            prepare(4 * i + 7)
+        for k in (2, 3):
+            raws[k][...] = out[k - 2]
+
+    def tiles_loop(half):
         def step(i, carry):
-            first = [multiply(4 * i + k, half) for k in (0, 1)]
-            for k in (2, 3):
-                finish(raws[k], (4 * i + k + 2 * TILES - 2) % (TILES + 1), half)
-            if half == 0:
-                prepare(4 * i + 4)
-                prepare(4 * i + 5)
-            for k in (0, 1):
-                raws[k][...] = first[k]
-            second = [multiply(4 * i + k, half) for k in (2, 3)]
-            for k in (0, 1):
-                finish(raws[k], 4 * i + k, half)
-            if half == 0:
-                prepare(4 * i + 6)
-                prepare(4 * i + 7)
-            for k in (2, 3):
-                raws[k][...] = second[k - 2]
+            four_tiles(i, half, half == 0)
             return carry
 
-        return step
+        lax.fori_loop(0, 2, step, 0)
 
     def to_partner(half):
         return pltpu.make_async_remote_copy(
@@ -384,11 +392,12 @@
 
     for k in range(4):
         prepare(jnp.int32(k))
-    lax.fori_loop(0, 3, four_tiles(0), 0)
+    tiles_loop(0)
+    four_tiles(2, 0, False)
     restore(0)
-    lax.fori_loop(0, 2, four_tiles(1), 0)
+    tiles_loop(1)
     send_far(0)
-    lax.fori_loop(2, 3, four_tiles(1), 0)
+    four_tiles(2, 1, False)
     restore(1)
     send_far(1)
     wait_far(0)
@@ -420,12 +429,12 @@
             pltpu.VMEM((144, 128, 128), F32),
             pltpu.VMEM((8, 1152, 256), BF16),
             pltpu.VMEM((8, 1152, 256), BF16),
-            pltpu.VMEM((TILES + 5, 256, 256), BF16),
-            pltpu.VMEM((TILES + 5, 256, 256), BF16),
-            pltpu.VMEM((TILES + 5, 2, 8, 128), F32),
+            pltpu.VMEM((TILES + 1, 256, 256), BF16),
+            pltpu.VMEM((TILES + 1, 256, 256), BF16),
+            pltpu.VMEM((TILES + 1, 2, 8, 128), F32),
             *[pltpu.VMEM((HALF * 8, 256), F32)] * 4,
             pltpu.VMEM((2, 4 * HALF, (TILES + 1) * 128), BF16),
-            pltpu.VMEM(((TILES + 5) * 128, 512), BF16),
+            pltpu.VMEM(((TILES + 1) * 128, 512), BF16),
             pltpu.VMEM((128, 1, 128), jnp.int32),
             pltpu.VMEM((512, 512), BF16),
             pltpu.VMEM((512, 512), BF16),

time: 40.1 us -> 39.4 us (0.983)
  Pallas kernels: 39.2 us -> 38.4 us
    pallas_call x1, Pallas kernels: 39.2 us -> 38.4 us  [vertices_kernel_call(): pl.pallas_call(program_kernel, out_shape=pltpu.VMEM((4, 288, 16), F32), i...]
where the time goes in v6:
time: 39.4 us; the launch traced here: 39.3 us
  Pallas kernels  38.4 us (97%)
  local copies, waits for them, and re-layouts  0.82 us (2%)
    pallas_call x1, Pallas kernels, vertices_kernel_call(): pl.pallas_call(program_kernel, out_shape=pltpu.VMEM((4, 288, 16), F32), i...  38.4 us
    unnamed x1, local copies, waits for them, and re-layouts  0.82 us

profile of v6, /device:TPU:1, one launch (start us, length us, event | category | flops | bytes accessed | tf_op | source)
XLA Modules:
  0.0 39.3 jit_solution(12718939046260315730)
XLA Ops:
  0.0 38.4 %shard_map.37 = f32[4,288,16]{2,1,0:T(8,128)S(1)} custom-call(f32[144,128,128]{2,1,0:T(8,128)} %bitcast.11, s32[4,4]{1,0:T(4,128)} %mom_smem.1, s32[16]{0:T(128)} %gamma_smem.1), custom_call_target="tpu_custom_call" | custom-call | tf_op jit(solution)/shard_map/pallas_call | solution.py:422
  38.5 0.8 %copy.6 = f32[4,16,2,12,12]{1,2,4,3,0:T(2,128)} copy(f32[4,16,2,12,12]{1,2,4,3,0:T(2,128)S(1)} %bitcast.10) | data formatting | bytes 147456

commit v7 on v6

--- a/solution.py
+++ b/solution.py
@@ -158,7 +158,7 @@
     x_hbm, mom_smem, gamma_smem, out_ref,
     sbuf, gh, gl, w_high, w_low, x_wave, raw_a, raw_b, raw_c, raw_d, yall, pick, mom_all,
     before_buf, move_buf, widen, slots,
-    zbuf, dbuf, hbuf, rbuf, spec,
+    zbuf, dbuf, hbuf, rbuf, own_out, own_in, spec,
     in_sems, mom_send, mom_recv, pair_send, pair_recv, far_send, far_recv, last_send, last_recv,
 ):
     gx, gz, ta = (lax.axis_index(name) for name in ("gx", "gz", "ta"))
@@ -373,22 +373,33 @@
             zbuf[half, part] = jnp.transpose(rows)
         to_partner(half).start()
 
-    def send_far(half):
+    def reduced(half):
         to_partner(half).wait_recv()
         total = (zbuf[half, core] + dbuf[half]) * (1.0 / math.sqrt(float(LX * LY * LZ * LT)))
-        hbuf[half] = total.reshape(64, 8, 128)
-        rbuf[half, chip] = hbuf[half, chip]
+        return total.reshape(64, 8, 128)
+
+    def send_first():
+        hbuf[...] = reduced(0)
+        rbuf[chip] = hbuf[chip]
         for place in chips[:-1]:
             pltpu.make_async_remote_copy(
-                src_ref=hbuf.at[half, chip_of(place)], dst_ref=rbuf.at[half, chip],
-                send_sem=far_send.at[half], recv_sem=far_recv.at[half],
+                src_ref=hbuf.at[chip_of(place)], dst_ref=rbuf.at[chip],
+                send_sem=far_send.at[0], recv_sem=far_recv.at[0],
                 device_id=device(place), device_id_type=MESH,
             ).start()
 
-    def wait_far(half):
-        blocks = rbuf.at[half, pl.ds(0, 63)]
-        pltpu.make_async_copy(blocks, blocks, far_recv.at[half]).wait()
-        spec[core, half] = jnp.sum(rbuf[half], axis=0)
+    def send_second():
+        total = reduced(1)
+        own_out[:, 0] = total[:, :4]
+        own_out[:, 1] = total[:, 4:]
+        own_in[core * 64 + chip] = own_out[chip, core]
+        for place, dc in others:
+            pltpu.make_async_remote_copy(
+                src_ref=own_out.at[chip_of(place), cores[dc]],
+                dst_ref=own_in.at[core * 64 + chip],
+                send_sem=far_send.at[1], recv_sem=far_recv.at[1],
+                device_id=device(place, dc), device_id_type=MESH,
+            ).start()
 
     for k in range(4):
         prepare(jnp.int32(k))
@@ -396,23 +407,30 @@
     four_tiles(2, 0, False)
     restore(0)
     tiles_loop(1)
-    send_far(0)
+    send_first()
     four_tiles(2, 1, False)
     restore(1)
-    send_far(1)
-    wait_far(0)
-    wait_far(1)
+    send_second()
+    blocks = rbuf.at[pl.ds(0, 63)]
+    owned = own_in.at[pl.ds(0, 127)]
+    pltpu.make_async_copy(blocks, blocks, far_recv.at[0]).wait()
+    spec[core, 0] = jnp.sum(rbuf[...], axis=0)
     last = pltpu.make_async_remote_copy(
-        src_ref=spec.at[core], dst_ref=spec.at[core], send_sem=last_send, recv_sem=last_recv,
+        src_ref=spec.at[core, 0], dst_ref=spec.at[core, 0],
+        send_sem=last_send, recv_sem=last_recv,
         device_id=device((0, 0, 0), 1), device_id_type=MESH,
     )
     last.start()
     pltpu.make_async_copy(all_rows, all_rows, mom_send).wait()
     for half in range(2):
         to_partner(half).wait_send()
-        blocks = hbuf.at[half, pl.ds(0, 63)]
-        pltpu.make_async_copy(blocks, blocks, far_send.at[half]).wait()
+    pltpu.make_async_copy(blocks, blocks, far_send.at[0]).wait()
     last.wait()
+    pltpu.make_async_copy(owned, owned, far_recv.at[1]).wait()
+    for part in range(2):
+        mine = jnp.sum(own_in[part * 64 : part * 64 + 64], axis=0)
+        spec[part, 1] = jnp.concatenate([mine, mine], axis=0)
+    pltpu.make_async_copy(owned, owned, far_send.at[1]).wait()
     write_vertices(spec, widen, slots, out_ref)
 
 
@@ -442,8 +460,10 @@
             pltpu.VMEM((256, 512), BF16),
             pltpu.VMEM((2, 2, 512, 128), F32),
             pltpu.VMEM((2, 512, 128), F32),
-            pltpu.VMEM((2, 64, 8, 128), F32),
-            pltpu.VMEM((2, 64, 8, 128), F32),
+            pltpu.VMEM((64, 8, 128), F32),
+            pltpu.VMEM((64, 8, 128), F32),
+            pltpu.VMEM((64, 2, 4, 128), F32),
+            pltpu.VMEM((128, 4, 128), F32),
             pltpu.VMEM((2, 2, 8, 128), F32),
             dma((CHUNKS,)),
             dma, dma, dma((2,)), dma((2,)), dma((2,)), dma((2,)), dma, dma,

time: 39.4 us -> 38.1 us (0.967)
  Pallas kernels: 38.4 us -> 37.1 us
    pallas_call x1, Pallas kernels: 38.4 us -> 37.1 us  [vertices_kernel_call(): pl.pallas_call(program_kernel, out_shape=pltpu.VMEM((4, 288, 16), F32), i...]
where the time goes in v7:
time: 38.1 us; the launch traced here: 38 us
  Pallas kernels  37.1 us (97%)
  local copies, waits for them, and re-layouts  0.82 us (2%)
    pallas_call x1, Pallas kernels, vertices_kernel_call(): pl.pallas_call(program_kernel, out_shape=pltpu.VMEM((4, 288, 16), F32), i...  37.1 us
    unnamed x1, local copies, waits for them, and re-layouts  0.82 us

profile of v7, /device:TPU:1, one launch (start us, length us, event | category | flops | bytes accessed | tf_op | source)
XLA Modules:
  0.0 38.0 jit_solution(3816541713253797126)
XLA Ops:
  0.0 37.1 %shard_map.37 = f32[4,288,16]{2,1,0:T(8,128)S(1)} custom-call(f32[144,128,128]{2,1,0:T(8,128)} %bitcast.11, s32[4,4]{1,0:T(4,128)} %mom_smem.1, s32[16]{0:T(128)} %gamma_smem.1), custom_call_target="tpu_custom_call" | custom-call | tf_op jit(solution)/shard_map/pallas_call | solution.py:440
  37.1 0.8 %copy.6 = f32[4,16,2,12,12]{1,2,4,3,0:T(2,128)} copy(f32[4,16,2,12,12]{1,2,4,3,0:T(2,128)S(1)} %bitcast.10) | data formatting | bytes 147456

commit v8 on v7

--- a/solution.py
+++ b/solution.py
@@ -104,30 +104,33 @@
     return out
 
 
-def write_vertices(spec, widen, slots, out_ref):
+def widened(spec, widen, half):
     keep = iota((8, 128), 1) < HALF
     lines = []
-    for sink in range(12):
-        half, k = divmod(sink, 6)
+    for k in range(6):
         for part in range(2):
             line = jnp.where(keep, spec[part, half], 0.0)
             lines.append(pltpu.roll(line, 128 - 12 * k, 1) if k else line)
     wide = jnp.concatenate(split(jnp.concatenate(lines, axis=0)), axis=1)
     wide = jnp.dot(wide, widen[...], preferred_element_type=F32)
     even = (iota((8, 384), 1) & 1) == 0
-    left_re = [wide[16 * k : 16 * k + 8, :384] for k in range(12)]
-    left_im = [wide[16 * k + 8 : 16 * k + 16, :384] for k in range(12)]
-    right, turned = [], []
-    for k in range(12):
-        re, im = wide[16 * k : 16 * k + 8, 384:], wide[16 * k + 8 : 16 * k + 16, 384:]
-        right.append(jnp.where(even, re, im))
-        turned.append(jnp.where(even, im, -re))
+    out = []
+    for k in range(6):
+        left_re, re = wide[16 * k : 16 * k + 8, :384], wide[16 * k : 16 * k + 8, 384:]
+        left_im, im = wide[16 * k + 8 : 16 * k + 16, :384], wide[16 * k + 8 : 16 * k + 16, 384:]
+        out.append((left_re, left_im, jnp.where(even, re, im), jnp.where(even, im, -re)))
+    return out
+
+
+def write_vertices(sinks, slots, out_ref):
+    even = (iota((8, 384), 1) & 1) == 0
 
     def pair(s, t):
         total = None
         for c in range(3):
-            a, b = 3 * s + c, 3 * t + c
-            term = left_re[a] * right[b] + left_im[a] * turned[b]
+            left_re, left_im = sinks[3 * s + c][:2]
+            right, turned = sinks[3 * t + c][2:]
+            term = left_re * right + left_im * turned
             total = term if total is None else total + term
         return total
 
@@ -426,12 +429,13 @@
         to_partner(half).wait_send()
     pltpu.make_async_copy(blocks, blocks, far_send.at[0]).wait()
     last.wait()
+    sinks = widened(spec, widen, 0)
     pltpu.make_async_copy(owned, owned, far_recv.at[1]).wait()
     for part in range(2):
         mine = jnp.sum(own_in[part * 64 : part * 64 + 64], axis=0)
         spec[part, 1] = jnp.concatenate([mine, mine], axis=0)
     pltpu.make_async_copy(owned, owned, far_send.at[1]).wait()
-    write_vertices(spec, widen, slots, out_ref)
+    write_vertices(sinks + widened(spec, widen, 1), slots, out_ref)
 
 
 def vertices_kernel_call(x, momenta, gamma_index):

time: 38.1 us -> 38 us (level)
  no operation moved by 1% of the time
where the time goes in v8:
time: 38 us; the launch traced here: 37.9 us
  Pallas kernels  37.1 us (98%)
  local copies, waits for them, and re-layouts  0.82 us (2%)
    pallas_call x1, Pallas kernels, vertices_kernel_call(): pl.pallas_call(program_kernel, out_shape=pltpu.VMEM((4, 288, 16), F32), i...  37.1 us
    unnamed x1, local copies, waits for them, and re-layouts  0.82 us

profile of v8, /device:TPU:1, one launch (start us, length us, event | category | flops | bytes accessed | tf_op | source)
XLA Modules:
  0.0 37.9 jit_solution(14382673017784097056)
XLA Ops:
  0.0 37.1 %shard_map.37 = f32[4,288,16]{2,1,0:T(8,128)S(1)} custom-call(f32[144,128,128]{2,1,0:T(8,128)} %bitcast.11, s32[4,4]{1,0:T(4,128)} %mom_smem.1, s32[16]{0:T(128)} %gamma_smem.1), custom_call_target="tpu_custom_call" | custom-call | tf_op jit(solution)/shard_map/pallas_call | solution.py:444
  37.1 0.8 %copy.6 = f32[4,16,2,12,12]{1,2,4,3,0:T(2,128)} copy(f32[4,16,2,12,12]{1,2,4,3,0:T(2,128)S(1)} %bitcast.10) | data formatting | bytes 147456

commit v9 on v8

--- a/solution.py
+++ b/solution.py
@@ -231,14 +231,14 @@
                     gl[q, rows, lanes] = rest[2 * q + part]
         return carry
 
-    lax.fori_loop(0, 10, fold_step, 0)
+    lax.fori_loop(0, 5, fold_step, 0)
     pl.semaphore_wait(barrier, 127)
     for place, dc in others:
         pltpu.make_async_remote_copy(
             src_ref=mom_all.at[me], dst_ref=mom_all.at[me], send_sem=mom_send, recv_sem=mom_recv,
             device_id=device(place, dc), device_id_type=MESH,
         ).start()
-    lax.fori_loop(10, CHUNKS, fold_step, 0)
+    lax.fori_loop(5, CHUNKS, fold_step, 0)
 
     before_buf[...] = (iota((512, 512), 0) < iota((512, 512), 1)).astype(F32).astype(BF16)
     to_row = iota((512, 512), 1)

time: 38 us -> 37.5 us (0.987)
  Pallas kernels: 37.1 us -> 36.6 us
    pallas_call x1, Pallas kernels: 37.1 us -> 36.6 us  [vertices_kernel_call(): pl.pallas_call(program_kernel, out_shape=pltpu.VMEM((4, 288, 16), F32), i...]
where the time goes in v9:
time: 37.5 us; the launch traced here: 37.4 us
  Pallas kernels  36.6 us (98%)
  local copies, waits for them, and re-layouts  0.82 us (2%)
    pallas_call x1, Pallas kernels, vertices_kernel_call(): pl.pallas_call(program_kernel, out_shape=pltpu.VMEM((4, 288, 16), F32), i...  36.6 us
    unnamed x1, local copies, waits for them, and re-layouts  0.82 us

profile of v9, /device:TPU:1, one launch (start us, length us, event | category | flops | bytes accessed | tf_op | source)
XLA Modules:
  0.0 37.4 jit_solution(7705234514971941085)
XLA Ops:
  0.0 36.6 %shard_map.37 = f32[4,288,16]{2,1,0:T(8,128)S(1)} custom-call(f32[144,128,128]{2,1,0:T(8,128)} %bitcast.11, s32[4,4]{1,0:T(4,128)} %mom_smem.1, s32[16]{0:T(128)} %gamma_smem.1), custom_call_target="tpu_custom_call" | custom-call | tf_op jit(solution)/shard_map/pallas_call | solution.py:444
  36.6 0.8 %copy.6 = f32[4,16,2,12,12]{1,2,4,3,0:T(2,128)} copy(f32[4,16,2,12,12]{1,2,4,3,0:T(2,128)S(1)} %bitcast.10) | data formatting | bytes 147456
